TPU v7x, 8 devices: a whole 2x2x1 slice. The times are simulated.
8 devices in a mesh: tp: 4 (over z, y, x), cp: 2 (over core).
Axes of the slice: x: 2, y: 2, z: 1, core: 2. Of those that a mesh axis runs over, the one named last changes fastest.
Arguments:
- x_in: bfloat16 [32, 256, 4096], P(None, 'cp')
- grad_z: bfloat16 [32, 256, 4096], P(None, 'cp')
- seg_pos: int32 [32, 256], P(None, 'cp')
- norm_scale: bfloat16 [4096], replicated
- w_x: bfloat16 [4096, 4096], P(None, 'tp')
- b_x: bfloat16 [4096], P('tp')
- w_y: bfloat16 [4096, 4096], P(None, 'tp')
- b_y: bfloat16 [4096], P('tp')
- conv_w: bfloat16 [4, 4096], P(None, 'tp')
- conv_b: bfloat16 [4096], P('tp')
- w_a: bfloat16 [16, 256, 256], P('tp')
- b_a: bfloat16 [4096], P('tp')
- w_i: bfloat16 [16, 256, 256], P('tp')
- b_i: bfloat16 [4096], P('tp')
- a_param: float32 [4096], P('tp')
- w_out: bfloat16 [4096, 4096], P('tp')
- b_out: bfloat16 [4096], replicated
Outputs:
- output 1: bfloat16 [32, 256, 4096], P(None, 'cp')
- output 2: bfloat16 [32, 256, 4096], P(None, 'cp')
- output 3: float32 [4096], replicated
- output 4: float32 [4096, 4096], P(None, 'tp')
- output 5: float32 [4096], P('tp')
- output 6: float32 [4096, 4096], P(None, 'tp')
- output 7: float32 [4096], P('tp')
- output 8: float32 [4, 4096], P(None, 'tp')
- output 9: float32 [4096], P('tp')
- output 10: float32 [16, 256, 256], P('tp')
- output 11: float32 [4096], P('tp')
- output 12: float32 [16, 256, 256], P('tp')
- output 13: float32 [4096], P('tp')
- output 14: float32 [4096], P('tp')
- output 15: float32 [4096, 4096], P('tp')
- output 16: float32 [4096], replicated
All inputs are finite; a program needn't handle non-finite values.
Results may differ from a plain program's by a relative error of at most 0.00874371.
Values sent between devices are 32-bit elements.
A program may use at most 1 GiB of HBM per device.

v0:
```python
import functools
import jax
import jax.numpy as jnp
from jax import lax
from jax.sharding import PartitionSpec as P

NORM_EPS = 1e-6
CONV_WIDTH = 4
BORROW_ROWS = CONV_WIDTH - 1
IN_SPECS = (P(None, "cp", None), P(None, "cp", None), P(None, "cp"), P(), P(None, "tp"), P("tp"), P(None, "tp"), P("tp"), P(None, "tp"), P("tp"), P("tp", None, None), P("tp"), P("tp", None, None), P("tp"), P("tp"), P("tp", None), P())
OUT_SPECS = (P(None, "cp", None), P(None, "cp", None), P(), P(None, "tp"), P("tp"), P(None, "tp"), P("tp"), P(None, "tp"), P("tp"), P("tp", None, None), P("tp"), P("tp", None, None), P("tp"), P("tp"), P("tp", None), P())


def norm_apply(x_f, scale_f):
    mean_sq = jnp.mean(x_f * x_f, axis=-1, keepdims=True)
    return x_f * lax.rsqrt(mean_sq + NORM_EPS) * (1.0 + scale_f)


def gelu_tanh(pre_y):
    return jax.nn.gelu(pre_y, approximate=True)


def gate_math(pre_a, pre_i, conv_f, a_param, reset_mask):
    log_a = -8.0 * jax.nn.sigmoid(pre_a) * jax.nn.softplus(a_param)
    decays = jnp.where(reset_mask, 0.0, jnp.exp(log_a))
    multiplier = jnp.where(reset_mask, 1.0, jnp.sqrt(-jnp.expm1(2.0 * log_a)))
    return decays, multiplier * jax.nn.sigmoid(pre_i) * conv_f


def conv_apply(xb_ext, conv_w, conv_b, pos_t):
    n_rows = pos_t.shape[0]
    conv_wf = conv_w.astype(jnp.float32)
    conv_sum = conv_b.astype(jnp.float32)
    for tap_k in range(CONV_WIDTH):
        start_row = BORROW_ROWS - tap_k
        keep_mask = (pos_t >= tap_k)[:, :, None]
        conv_sum = conv_sum + jnp.where(keep_mask, xb_ext[start_row:start_row + n_rows], 0.0) * conv_wf[tap_k]
    return conv_sum


def conv_back(grad_conv, xb_ext, conv_w, pos_t):
    n_rows = pos_t.shape[0]
    conv_wf = conv_w.astype(jnp.float32)
    grad_ext = 0.0
    tap_grads = []
    for tap_k in range(CONV_WIDTH):
        start_row = BORROW_ROWS - tap_k
        masked = jnp.where((pos_t >= tap_k)[:, :, None], grad_conv, 0.0)
        tap_grads.append(jnp.sum(masked * xb_ext[start_row:start_row + n_rows], axis=(0, 1)))
        grad_ext = grad_ext + jnp.pad(masked * conv_wf[tap_k], ((start_row, tap_k), (0, 0), (0, 0)))
    return grad_ext, jnp.stack(tap_grads), jnp.sum(grad_conv, axis=(0, 1))


def local_scan(decays, drives):
    def scan_step(carry_in, inputs_t):
        state_h, prod_a = carry_in
        state_h = inputs_t[0] * state_h + inputs_t[1]
        prod_a = inputs_t[0] * prod_a
        return (state_h, prod_a), (state_h, prod_a)
    zeros_h = jnp.zeros(decays.shape[1:], jnp.float32)
    _, (states, run_prods) = lax.scan(scan_step, (zeros_h, jnp.ones_like(zeros_h)), (decays, drives))
    return states, run_prods


def local_scan_back(decays, grad_out):
    def scan_step(carry_in, inputs_t):
        next_grad, prod_a = carry_in
        grad_h = inputs_t[1] + next_grad
        return (inputs_t[0] * grad_h, inputs_t[0] * prod_a), (grad_h, prod_a)
    zeros_h = jnp.zeros(decays.shape[1:], jnp.float32)
    (head_grad, total_prod), (grad_loc, suffix_prods) = lax.scan(scan_step, (zeros_h, jnp.ones_like(zeros_h)), (decays, grad_out), reverse=True)
    return grad_loc, suffix_prods, head_grad, total_prod


def carry_in_forward(end_info, cp_index):
    def compose(carry_in, piece_info):
        return piece_info[0] * carry_in + piece_info[1], carry_in
    _, entering = lax.scan(compose, jnp.zeros_like(end_info[0, 0]), end_info)
    return lax.dynamic_index_in_dim(entering, cp_index, 0, keepdims=False)


def carry_in_backward(head_info, cp_index):
    def compose(carry_in, piece_info):
        return piece_info[0] * carry_in + piece_info[1], carry_in
    _, entering = lax.scan(compose, jnp.zeros_like(head_info[0, 0]), head_info, reverse=True)
    return lax.dynamic_index_in_dim(entering, cp_index, 0, keepdims=False)


def shard_body(x_in, grad_z, seg_pos, norm_scale, w_x, b_x, w_y, b_y, conv_w, conv_b, w_a, b_a, w_i, b_i, a_param, w_out, b_out, fwd_perm, back_perm):
    cp_index = lax.axis_index("cp")
    n_tok = x_in.shape[1]
    n_blocks, blk_width = w_a.shape[0], w_a.shape[1]
    x_f = x_in.astype(jnp.float32)
    normed_f, norm_pull = jax.vjp(norm_apply, x_f, norm_scale.astype(jnp.float32))
    normed = normed_f.astype(jnp.bfloat16)
    pre_y = jnp.einsum("btd,dl->tbl", normed, w_y, preferred_element_type=jnp.float32) + b_y
    y_act, gelu_pull = jax.vjp(gelu_tanh, pre_y)
    x_branch = (jnp.einsum("btd,dl->tbl", normed, w_x, preferred_element_type=jnp.float32) + b_x).astype(jnp.bfloat16).astype(jnp.float32)
    borrowed = lax.ppermute(x_branch[n_tok - BORROW_ROWS:], "cp", fwd_perm)
    xb_ext = jnp.concatenate([borrowed, x_branch], axis=0)
    pos_t = seg_pos.T
    conv_out = conv_apply(xb_ext, conv_w, conv_b, pos_t).astype(jnp.bfloat16)
    blocks = conv_out.reshape(conv_out.shape[0], conv_out.shape[1], n_blocks, blk_width)
    pre_a = jnp.einsum("tbhk,hkj->tbhj", blocks, w_a, preferred_element_type=jnp.float32).reshape(conv_out.shape) + b_a
    pre_i = jnp.einsum("tbhk,hkj->tbhj", blocks, w_i, preferred_element_type=jnp.float32).reshape(conv_out.shape) + b_i
    gate_fn = functools.partial(gate_math, reset_mask=(pos_t == 0)[:, :, None])
    (decays, drives), gate_pull = jax.vjp(gate_fn, pre_a, pre_i, conv_out.astype(jnp.float32), a_param)
    states, run_prods = local_scan(decays, drives)
    end_info = lax.all_gather(jnp.stack([run_prods[-1], states[-1]]), "cp")
    state_in = carry_in_forward(end_info, cp_index)
    hidden = states + run_prods * state_in
    prev_hidden = jnp.concatenate([state_in[None], hidden[:-1]], axis=0)
    mixed_v = (hidden * y_act).astype(jnp.bfloat16)
    out_part = jnp.einsum("tbl,ld->btd", mixed_v, w_out, preferred_element_type=jnp.float32)
    out_proj = lax.psum(out_part, "tp") + b_out
    z_out = (x_f + out_proj).astype(jnp.bfloat16)

    d_mixed = jnp.einsum("btd,ld->tbl", grad_z, w_out, preferred_element_type=jnp.float32)
    g_w_out = jnp.einsum("tbl,btd->ld", mixed_v, grad_z, preferred_element_type=jnp.float32)
    g_b_out = jnp.sum(grad_z, axis=(0, 1), dtype=jnp.float32)
    d_pre_y = gelu_pull(d_mixed * hidden)[0]
    grad_loc, suffix_prods, head_grad, total_prod = local_scan_back(decays, d_mixed * y_act)
    head_info = lax.all_gather(jnp.stack([total_prod, head_grad]), "cp")
    grad_in = carry_in_backward(head_info, cp_index)
    d_hidden = grad_loc + suffix_prods * grad_in
    d_pre_a, d_pre_i, d_conv_f, g_a_param = gate_pull((d_hidden * prev_hidden, d_hidden))
    d_pre_a16 = d_pre_a.astype(jnp.bfloat16).reshape(blocks.shape)
    d_pre_i16 = d_pre_i.astype(jnp.bfloat16).reshape(blocks.shape)
    g_w_a = jnp.einsum("tbhk,tbhj->hkj", blocks, d_pre_a16, preferred_element_type=jnp.float32)
    g_w_i = jnp.einsum("tbhk,tbhj->hkj", blocks, d_pre_i16, preferred_element_type=jnp.float32)
    d_gate_in = jnp.einsum("tbhj,hkj->tbhk", d_pre_a16, w_a, preferred_element_type=jnp.float32) + jnp.einsum("tbhj,hkj->tbhk", d_pre_i16, w_i, preferred_element_type=jnp.float32)
    d_conv = d_conv_f + d_gate_in.reshape(conv_out.shape)
    grad_ext, g_conv_w, g_conv_b = conv_back(d_conv, xb_ext, conv_w, pos_t)
    returned = lax.ppermute(grad_ext[:BORROW_ROWS], "cp", back_perm)
    d_branch = jnp.concatenate([grad_ext[BORROW_ROWS:n_tok], grad_ext[n_tok:] + returned], axis=0)
    d_branch16 = d_branch.astype(jnp.bfloat16)
    d_pre_y16 = d_pre_y.astype(jnp.bfloat16)
    g_w_x = jnp.einsum("btd,tbl->dl", normed, d_branch16, preferred_element_type=jnp.float32)
    g_w_y = jnp.einsum("btd,tbl->dl", normed, d_pre_y16, preferred_element_type=jnp.float32)
    d_norm_part = jnp.einsum("tbl,dl->btd", d_branch16, w_x, preferred_element_type=jnp.float32) + jnp.einsum("tbl,dl->btd", d_pre_y16, w_y, preferred_element_type=jnp.float32)
    d_normed = lax.psum(d_norm_part, "tp")
    d_x_norm, g_scale = norm_pull(d_normed)
    grad_x = (grad_z.astype(jnp.float32) + d_x_norm).astype(jnp.bfloat16)
    grad_sums = lax.psum((g_scale, g_w_x, jnp.sum(d_branch, axis=(0, 1)), g_w_y, jnp.sum(d_pre_y, axis=(0, 1)), g_conv_w, g_conv_b, g_w_a, jnp.sum(d_pre_a, axis=(0, 1)), g_w_i, jnp.sum(d_pre_i, axis=(0, 1)), g_a_param, g_w_out, g_b_out), "cp")
    return (z_out, grad_x) + tuple(grad_sums)


def solution(mesh):
    cp_size = mesh.shape["cp"]
    fwd_perm = [(dev_j, dev_j + 1) for dev_j in range(cp_size - 1)]
    back_perm = [(dev_j + 1, dev_j) for dev_j in range(cp_size - 1)]
    per_device = functools.partial(shard_body, fwd_perm=fwd_perm, back_perm=back_perm)
    return jax.shard_map(per_device, mesh=mesh, in_specs=IN_SPECS, out_specs=OUT_SPECS, check_vma=False)
```

profile of v0, /device:TPU:0, one launch (start us, length us, event | category | flops | bytes accessed | tf_op | source)
XLA Modules:
  0.0 4831.9 jit_solution(2547169674938873259)
XLA Ops:
  19.3 42.7 add_convert_fusion.1
  78.9 43.3 fusion.36
  122.8 49.1 %bitcast_multiply_fusion.5 = (f32[128,32,1024]{2,0,1:T(8,128)}, f32[1024,32,128]{0,2,1:T(8,128)}) fusion(f32[32,128,1024]{2,1,0:T(8,128)} %fusion.36, f32[1024]{0:T(1024)S(1)} %convert_element_type.91, bf16[32,128,4096]{2,1,0:T(8,128)(2,1)} %param.26, bf16[1024,4096]{1,0:T(8,128)(2,1)} %param.40), kind=kOutput, calls=%fused_computation.69 | convolution fusion | flops 34401681408 | bytes 92278784 | tf_op jit(solution)/shard_map/btd,ld->tbl/dot_general | solution.py:118
  172.1 34.8 add_convert_fusion
  206.9 14.6 reshape.97
  221.5 13.9 copy.82
  261.8 19.5 copy.66
  297.3 1278.5 %while.70 = (s32[]{:T(128)}, f32[32,1024]{1,0:T(8,128)S(1)}, f32[32,1024]{1,0:T(8,128)S(1)}, f32[128,32,1024]{2,0,1:T(8,128)}, f32[128,32,1024]{2,0,1:T(8,128)},...) while((s32[]{:T(128)}, f32[32,1024]{1,0:T(8,128)S(1)}, ...), condition=%wide.region_7.8_spmd.clone, body=%wide.region_6.7_spmd.clone.sunk | while | flops 163844 | bytes 2359435 | solution.py:71
  1578.2 12.7 convolution_bitcast_fusion.2
  1602.9 44.4 fusion.86
  1647.3 393.1 %while.68 = (s32[]{:T(128)}, f32[32,1024]{1,0:T(8,128)S(1)}, f32[32,1024]{1,0:T(8,128)S(1)}, f32[128,32,1024]{2,1,0:T(8,128)}, f32[128,32,1024]{2,1,0:T(8,128)},...) while((s32[]{:T(128)}, f32[32,1024]{1,0:T(8,128)S(1)}, ...), condition=%wide.region_2.3_spmd.clone, body=%wide.region_1.2_spmd.clone.sunk | while | flops 163843 | bytes 1311339 | solution.py:61
  2047.2 43.0 fusion.89
  2090.2 39.2 multiply_reduce_fusion
  2129.4 12.4 fusion.67
  2153.7 16.7 add_bitcast_fusion.1
  2182.6 50.8 %fusion.84 = (f32[1024]{0:T(1024)}, f32[1024]{0:T(1024)}, f32[1024]{0:T(1024)}, f32[1024]{0:T(1024)}, f32[1024]{0:T(1024)}, /*index=5*/f32[128,32,1024]{2,0,1:T(8,128)}) fusion(bf16[32,128,1024]{2,1,0:T(8,128)(2,1)} %add_convert_fusion.1, pred[128,32]{0,1:T(8,128)(4,1)S(1)} %copy-done.28, f32[128,32,1024]{2,0,1:T(8,128)} %convert_bitcast_fusion, ...), kind=kLoop, calls=%fused_computation.164 | loop fusion | flops 134212608 | bytes 109498368 | tf_op jit(solution)/shard_map/reduce_sum | solution.py:51
  2233.4 27.0 select_multiply_fusion.3
  2263.9 45.8 fusion.55
  2309.7 30.0 pad_add_fusion
  2353.0 61.1 %add_bitcast_fusion = f32[32,128,4096]{2,1,0:T(8,128)} fusion(f32[128,32,4096]{2,0,1:T(8,128)} %fusion.55, bf16[4096,1024]{1,0:T(8,128)(2,1)} %param.29, bf16[3,32,1024]{2,0,1:T(4,128)(2,1)S(1)} %get-tuple-element.501, bf16[125,32,1024]{2,0,1:T(8,128)(2,1)} %slice.136), kind=kOutput, calls=%fused_computation.40 | convolution fusion | flops 34393292800 | bytes 150994944 | tf_op jit(solution)/shard_map/tbl,dl->btd/dot_general | solution.py:140
  2414.8 15.4 multiply_convert_fusion
  2430.2 45.5 convolution_bitcast_fusion
  2494.4 42.5 convolution_bitcast_fusion.1
  2537.0 43.9 fusion.42
  2580.9 45.0 fusion.39
  2636.4 885.7 %all-reduce.13.cloned.1.call-done = f32[32,128,4096]{2,1,0:T(8,128)} async-done(((f32[32,128,4096]{2,1,0:T(8,128)}), f32[32,128,4096]{2,1,0:T(8,128)}) %all-reduce.13.cloned.1.call-update) | async-done | bytes 67108880 | tf_op jit(solution)/shard_map/psum | solution.py:141
  3522.0 32.4 fusion.10
  3554.5 1077.6 %all-reduce.11.cloned.1.call-done = f32[32,128,4096]{2,1,0:T(8,128)} async-done(((f32[32,128,4096]{2,1,0:T(8,128)}), f32[32,128,4096]{2,1,0:T(8,128)}) %all-reduce.11.cloned.1.call-update) | async-done | bytes 67108880 | tf_op jit(solution)/shard_map/psum | solution.py:115
  4632.1 85.4 %convert_reduce_fusion = (f32[4096]{0:T(1024)}, bf16[32,128,4096]{2,1,0:T(8,128)(2,1)}, bf16[32,128,4096]{2,1,0:T(8,128)(2,1)}) fusion(bf16[32,128,4096]{2,1,0:T(8,128)(2,1)} %param.26, f32[32,128]{1,0:T(8,128)S(1)} %multiply_multiply_fusion.2, bf16[32,128,4096]{2,1,0:T(8,128)(2,1)} %param.25, f32[32,128]{1,0:T(8,128)S(1)} %copy-done.22, ...), kind=kLoop, calls=%fused_computation.30 | loop fusion | flops 218099712 | bytes 268517376 | tf_op jit(solution)/shard_map/reduce_sum | solution.py:120
  4717.5 49.8 %all-reduce.17.cloned.1.call-done = (f32[4096,1024]{1,0:T(8,128)}, f32[4096,1024]{1,0:T(8,128)}, f32[4,256,256]{2,1,0:T(8,128)}, f32[4,256,256]{2,1,0:T(8,128)}, f32[1024,4096]{1,0:T(8,128)}) async-done(((f32[4096,1024]{1,0:T(8,128)}, f32[4096,1024]{1,0:T(8,128)}, f32[4,256,256]{2,1,0:T(8,128)}, f32[4,256,256]{2,1,0:T(8,128)}, f32[1024,4096]{1,0:T(8,128)}), (f32[4096,1024]{1,0:T(8,128)}, ...) | async-done | bytes 52428816 | tf_op jit(solution)/shard_map/psum | solution.py:144
  4767.3 18.8 all-reduce.15.cloned.1.call-done
  4787.5 13.7 copy.243
  (1271 shorter events, 1858.1 us)
Async XLA Ops:
  7.2 228.2 %copy-start = (bf16[4,256,256]{2,1,0:T(8,128)(2,1)S(1)}, bf16[4,256,256]{2,1,0:T(8,128)(2,1)}, u32[]{:S(2)}) copy-start(bf16[4,256,256]{2,1,0:T(8,128)(2,1)} %param.35) | copy-start | bytes 1572868
  7.2 3514.8 %all-reduce.13.cloned.1.call-start = ((), (), s32[]{:S(2)}) async-start(), calls=%async_computation.1 | async-start | bytes 134217728 | tf_op jit(solution)/shard_map/psum | solution.py:141
  19.3 59.6 %copy-start.21 = (f32[32,128]{1,0:T(8,128)}, f32[32,128]{1,0:T(8,128)S(1)}, u32[]{:S(2)}) copy-start(f32[32,128]{1,0:T(8,128)S(1)} %fusion.78) | copy-start | bytes 49156
  19.3 59.6 %copy-start.23 = (f32[4096]{0:T(1024)}, f32[4096]{0:T(1024)S(1)}, u32[]{:S(2)}) copy-start(f32[4096]{0:T(1024)S(1)} %convert_add_fusion.2) | copy-start | bytes 49156
  74.8 97.2 %collective-permute-start = (f32[3,32,1024]{2,0,1:T(4,128)S(1)}, f32[3,32,1024]{2,0,1:T(4,128)S(1)}, u32[]{:S(2)}, u32[]{:S(2)}) collective-permute-start(f32[3,32,1024]{2,0,1:T(4,128)S(1)} %slice.96), channel_id=1, source_target_pairs={{0,1},{2,3},{4,5},{6,7}} | collective-permute-start | bytes 1179656 | tf_op jit(solution)/shard_map/ppermute | solution.py:99
  78.3 93.8 %copy-start.35 = (f32[1,1024]{1,0:T(1,128)}, f32[1,1024]{1,0:T(1,128)S(1)}, u32[]{:S(2)}) copy-start(f32[1,1024]{1,0:T(1,128)S(1)} %get-tuple-element.523) | copy-start | bytes 12292
  78.3 93.8 %copy-start.37 = (f32[1,1024]{1,0:T(1,128)}, f32[1,1024]{1,0:T(1,128)S(1)}, u32[]{:S(2)}) copy-start(f32[1,1024]{1,0:T(1,128)S(1)} %get-tuple-element.524) | copy-start | bytes 12292
  78.3 93.8 %copy-start.39 = (f32[1,1024]{1,0:T(1,128)}, f32[1,1024]{1,0:T(1,128)S(1)}, u32[]{:S(2)}) copy-start(f32[1,1024]{1,0:T(1,128)S(1)} %get-tuple-element.525) | copy-start | bytes 12292
  78.3 93.8 %copy-start.41 = (f32[1,1024]{1,0:T(1,128)}, f32[1,1024]{1,0:T(1,128)S(1)}, u32[]{:S(2)}) copy-start(f32[1,1024]{1,0:T(1,128)S(1)} %get-tuple-element.526) | copy-start | bytes 12292
  122.2 1925.0 %copy-start.43 = (f32[1024]{0:T(1024)}, f32[1024]{0:T(1024)S(1)}, u32[]{:S(2)}) copy-start(f32[1024]{0:T(1024)S(1)} %convert_element_type.91) | copy-start | bytes 12292
  122.8 49.1 %copy-start.52 = (f32[1024]{0:T(1024)S(1)}, f32[1024]{0:T(1024)}, u32[]{:S(2)}) copy-start(f32[1024]{0:T(1024)} %param.39) | copy-start | bytes 12292
  122.8 49.1 %copy-start.54 = (s32[32,128]{1,0:T(8,128)S(1)}, s32[32,128]{1,0:T(8,128)}, u32[]{:S(2)}) copy-start(s32[32,128]{1,0:T(8,128)} %param.27) | copy-start | bytes 49156
  172.0 49.5 %copy-start.27 = (pred[128,32]{0,1:T(8,128)(4,1)}, pred[128,32]{0,1:T(8,128)(4,1)S(1)}, u32[]{:S(2)}) copy-start(pred[128,32]{0,1:T(8,128)(4,1)S(1)} %get-tuple-element.518) | copy-start | bytes 12292
  172.0 49.5 %copy-start.29 = (pred[128,32]{0,1:T(8,128)(4,1)}, pred[128,32]{0,1:T(8,128)(4,1)S(1)}, u32[]{:S(2)}) copy-start(pred[128,32]{0,1:T(8,128)(4,1)S(1)} %get-tuple-element.519) | copy-start | bytes 12292
  172.0 49.5 %copy-start.31 = (pred[128,32]{0,1:T(8,128)(4,1)}, pred[128,32]{0,1:T(8,128)(4,1)S(1)}, u32[]{:S(2)}) copy-start(pred[128,32]{0,1:T(8,128)(4,1)S(1)} %get-tuple-element.521) | copy-start | bytes 12292
  172.0 49.4 %copy-start.33 = (pred[128,32]{0,1:T(8,128)(4,1)}, pred[128,32]{0,1:T(8,128)(4,1)S(1)}, u32[]{:S(2)}) copy-start(pred[128,32]{0,1:T(8,128)(4,1)S(1)} %get-tuple-element.522) | copy-start | bytes 12292
  172.0 49.4 %copy-start.11 = (f32[3,32,1024]{2,0,1:T(4,128)}, f32[3,32,1024]{2,0,1:T(4,128)S(1)}, u32[]{:S(2)}) copy-start(f32[3,32,1024]{2,0,1:T(4,128)S(1)} %collective-permute-done) | copy-start | bytes 1179652
  289.3 1288.7 %copy-start.5 = (f32[32,1024]{1,0:T(8,128)S(1)}, f32[32,1024]{1,0:T(8,128)}, u32[]{:S(2)}) copy-start(f32[32,1024]{1,0:T(8,128)} %custom-call.5) | copy-start | bytes 393220
  289.3 1288.9 %copy-start.13 = (bf16[4,256,256]{2,1,0:T(8,128)(2,1)S(1)}, bf16[4,256,256]{2,1,0:T(8,128)(2,1)}, u32[]{:S(2)}) copy-start(bf16[4,256,256]{2,1,0:T(8,128)(2,1)} %param.37) | copy-start | bytes 1572868
  1602.9 441.6 %copy-start.10 = (f32[32,1024]{1,0:T(8,128)S(1)}, f32[32,1024]{1,0:T(8,128)}, u32[]{:S(2)}) copy-start(f32[32,1024]{1,0:T(8,128)} %custom-call.2) | copy-start | bytes 393220
  1602.9 441.6 %copy-start.26 = (f32[2,32,1024]{2,0,1:T(2,128)S(1)}, f32[2,32,1024]{2,0,1:T(2,128)}, u32[]{:S(2)}) copy-start(f32[2,32,1024]{2,0,1:T(2,128)} %custom-call.8) | copy-start | bytes 786436
  2182.5 50.9 %copy-start.36 = (f32[1,1024]{1,0:T(1,128)S(1)}, f32[1,1024]{1,0:T(1,128)}, u32[]{:S(2)}) copy-start(f32[1,1024]{1,0:T(1,128)} %copy-done.35) | copy-start | bytes 12292
  2182.6 50.9 %copy-start.38 = (f32[1,1024]{1,0:T(1,128)S(1)}, f32[1,1024]{1,0:T(1,128)}, u32[]{:S(2)}) copy-start(f32[1,1024]{1,0:T(1,128)} %copy-done.37) | copy-start | bytes 12292
  2182.6 50.9 %copy-start.40 = (f32[1,1024]{1,0:T(1,128)S(1)}, f32[1,1024]{1,0:T(1,128)}, u32[]{:S(2)}) copy-start(f32[1,1024]{1,0:T(1,128)} %copy-done.39) | copy-start | bytes 12292
  2182.6 50.8 %copy-start.42 = (f32[1,1024]{1,0:T(1,128)S(1)}, f32[1,1024]{1,0:T(1,128)}, u32[]{:S(2)}) copy-start(f32[1,1024]{1,0:T(1,128)} %copy-done.41) | copy-start | bytes 12292
  2262.6 87.4 %collective-permute-start.1 = (f32[3,32,1024]{2,0,1:T(4,128)S(1)}, f32[3,32,1024]{2,0,1:T(4,128)S(1)}, u32[]{:S(2)}, u32[]{:S(2)}) collective-permute-start(f32[3,32,1024]{2,0,1:T(4,128)S(1)} %pad_add_fusion.1), channel_id=1, source_target_pairs={{1,0},{3,2},{5,4},{7,6}} | collective-permute-start | bytes 1179656 | tf_op jit(solution)/shard_map/ppermute | solution.py:134
  2353.0 61.1 %copy-start.16 = (bf16[3,32,1024]{2,0,1:T(4,128)(2,1)}, bf16[3,32,1024]{2,0,1:T(4,128)(2,1)S(1)}, u32[]{:S(2)}) copy-start(bf16[3,32,1024]{2,0,1:T(4,128)(2,1)S(1)} %get-tuple-element.501) | copy-start | bytes 589828
  2414.1 2218.0 %all-reduce.11.cloned.1.call-start = ((), (), s32[]{:S(2)}) async-start(), calls=%async_computation | async-start | bytes 134217728 | tf_op jit(solution)/shard_map/psum | solution.py:115
  2475.7 2291.6 %all-reduce.17.cloned.1.call-start = ((), (), s32[]{:S(2)}) async-start(), calls=%async_computation.3 | async-start | bytes 104857600 | tf_op jit(solution)/shard_map/psum | solution.py:144
  2485.2 51.8 %slice-start.4 = ((s8[8388608]{0:T(1024)(128)(4,1)}), s8[4194304]{0:T(1024)(128)(4,1)S(1)}, s32[]{:S(2)}) async-start(s8[8388608]{0:T(1024)(128)(4,1)} %bitcast.230), calls=%async_computation.8 | async-start | bytes 8388608
  2625.9 2160.2 %all-reduce.15.cloned.1.call-start = ((), (), s32[]{:S(2)}) async-start(), calls=%async_computation.2 | async-start | bytes 147456 | tf_op jit(solution)/shard_map/psum | solution.py:144
  2636.4 918.1 %copy-start.20 = (f32[32,128]{1,0:T(8,128)S(1)}, f32[32,128]{1,0:T(8,128)}, u32[]{:S(2)}) copy-start(f32[32,128]{1,0:T(8,128)} %copy-done.19) | copy-start | bytes 49156
  (52 other events, 807.4 us)
Sparse Core Ops, SparseCore 0:
  2414.2 1107.7 all-reduce.12
  3525.5 1106.5 all-reduce.10
  4636.2 131.0 all-reduce.16
  4771.3 14.8 all-reduce.14
where the time goes:
time: 4870 us; the launch traced here: 4830 us
  waiting for transfers between devices  2030 us (42%)
  local copies, waits for them, and re-layouts  1470 us (30%)
  other arithmetic  813 us (17%)
  matrix products  488 us (10%)
    psum x1, waiting for transfers between devices, shard_body(): out_proj = lax.psum(out_part, 'tp') + b_out  1080 us
    dynamic_update_slice x512, local copies, waits for them, and re-layouts, local_scan(): lax.scan(scan_step, (zeros_h, jnp.ones_like(zeros_h)), (decays, drives))  977 us
    psum x1, waiting for transfers between devices, shard_body(): d_normed = lax.psum(d_norm_part, 'tp')  886 us
    dynamic_slice x256, local copies, waits for them, and re-layouts, local_scan(): lax.scan(scan_step, (zeros_h, jnp.ones_like(zeros_h)), (decays, drives))  338 us
    dynamic_update_slice x128, other arithmetic, local_scan(): lax.scan(scan_step, (zeros_h, jnp.ones_like(zeros_h)), (decays, drives))  223 us
    mul x128, other arithmetic, scan_step(): return ((inputs_t[0] * grad_h, inputs_t[0] * prod_a), (grad_h, prod_a))  129 us
  transfers between devices with their start and end apart: 6, of which 4 were waited for; matrix products, arithmetic and copies ran while one was open for 11% of the time, Pallas kernels for 0%

commit v1 on v0

v1 whole, which is shorter than its diff:
```python
import functools
import jax
import jax.numpy as jnp
from jax import lax
from jax.experimental import pallas as pl
from jax.experimental.pallas import tpu as pltpu
from jax.sharding import PartitionSpec as P

NORM_EPS = 1e-6
TINY, FAR = 1e-37, 1e4
LOG2E = 1.4426950408889634
GELU_K0 = 0.7978845608028654
GELU_K1 = GELU_K0 * 0.044715
SUB = 8
TOK, GRP, CH, DM, LANES, TILE = 128, 4, 256, 4096, 128, 16
GROWS = TOK * SUB
ROWS = GRP * GROWS
HALF = DM // 2
PIECE, HALO = 256, 32
KSTEP, STRIP = 1024, 32
POS_ROWS = GROWS + 64
COLS = DM // LANES
BF, F32 = jnp.bfloat16, jnp.float32
ANY = pl.BlockSpec(memory_space=pl.ANY)
VM = pl.BlockSpec(memory_space=pltpu.VMEM)
VMEM_MOST = 67000000
NT = (((1,), (1,)), ((), ()))
TN = (((0,), (0,)), ((), ()))
SEQ, ALL, CHAN, COL, BLK, ROW = P(None, "cp", None), P(), P("tp"), P(None, "tp"), P("tp", None, None), P("tp", None)
PARAMS = (COL, CHAN, COL, CHAN, COL, CHAN, BLK, CHAN, BLK, CHAN, CHAN, ROW, ALL)
IN_SPECS = (SEQ, SEQ, P(None, "cp"), ALL) + PARAMS
OUT_SPECS = (SEQ, SEQ, ALL) + PARAMS


def sds(shape, dtype):
    return jax.ShapeDtypeStruct(shape, dtype)


TOKEN = sds((SUB, LANES), F32)


def cost(us):
    return pl.CostEstimate(flops=int(us * 1e9), bytes_accessed=int(us * 1e6), transcendentals=0)


def params(**kw):
    return pltpu.CompilerParams(vmem_limit_bytes=VMEM_MOST, **kw)


def lane_tiles():
    return [(j, slice(j * LANES, (j + 1) * LANES)) for j in range(COLS)]


NTOK = TOK // TILE
SEQ_BLOCK = pl.BlockSpec((SUB, TILE, DM), lambda g, t: (g, t, 0))
ROW_BLOCK = pl.BlockSpec((SUB * TILE, DM), lambda g, t: (g * NTOK + t, 0))
ONE_ROW = pl.BlockSpec((1, DM), lambda g, t: (0, 0))
SUM_BLOCK = pl.BlockSpec((SUB, DM), lambda g, t: (0, 0))
TURN = pltpu.VMEM((COLS, SUB * TILE, LANES), F32)


def row_call(kernel, us, inputs, in_specs, out_specs, out_shape, turns):
    return pl.pallas_call(kernel, grid=(GRP, NTOK), in_specs=in_specs, out_specs=out_specs, out_shape=out_shape, scratch_shapes=[TURN] * turns,
                          compiler_params=params(), cost_estimate=cost(us))(*inputs)


def first_step():
    return (pl.program_id(0) == 0) & (pl.program_id(1) == 0)


def both(val):
    return val[:SUB] + val[SUB:]


def row_scales(x_ref, more=None):
    found = []
    for b in range(SUB):
        square = other = jnp.zeros((TILE, LANES), F32)
        for j, cols in lane_tiles():
            xf = x_ref[b, :, cols].astype(F32)
            square = square + xf * xf
            if more is not None:
                other = other + xf * more(b, j, cols)
        rstd = lax.rsqrt(jnp.sum(square, axis=-1, keepdims=True) * (1.0 / DM) + NORM_EPS)
        found.append((rstd, jnp.sum(other, axis=-1, keepdims=True) * (1.0 / DM)))
    return found


def norm_kernel(x_ref, gz_ref, sc_ref, n_ref, g_ref, gb_ref, sn_ref, sg_ref):
    @pl.when(first_step())
    def _():
        gb_ref[...] = jnp.zeros_like(gb_ref)

    rows = row_scales(x_ref)
    for j, cols in lane_tiles():
        scale = 1.0 + sc_ref[:, cols]
        total = gb_ref[:, cols]
        for b in range(SUB):
            gf = gz_ref[b, :, cols].astype(F32)
            total = total + both(gf)
            sn_ref[j, pl.ds(b, TILE, stride=SUB), :] = x_ref[b, :, cols].astype(F32) * rows[b][0] * scale
            sg_ref[j, pl.ds(b, TILE, stride=SUB), :] = gf
        gb_ref[:, cols] = total
        n_ref[:, cols] = sn_ref[j].astype(BF)
        g_ref[:, cols] = sg_ref[j].astype(BF)


def norm_call(x, gz, scale):
    return row_call(norm_kernel, 60, (x, gz, scale), [SEQ_BLOCK, SEQ_BLOCK, ONE_ROW], [ROW_BLOCK, ROW_BLOCK, SUM_BLOCK],
                    [sds((ROWS, DM), BF), sds((ROWS, DM), BF), sds((SUB, DM), F32)], 2)


def z_kernel(acc_ref, x_ref, bo_ref, z_ref, sa_ref):
    for j, cols in lane_tiles():
        sa_ref[j] = acc_ref[:, cols]
    for b in range(SUB):
        for j, cols in lane_tiles():
            z_ref[b, :, cols] = (x_ref[b, :, cols].astype(F32) + (sa_ref[j, pl.ds(b, TILE, stride=SUB), :] + bo_ref[:, cols])).astype(BF)


def z_call(acc, x, b_out):
    return row_call(z_kernel, 50, (acc, x, b_out), [ROW_BLOCK, SEQ_BLOCK, ONE_ROW], SEQ_BLOCK, sds((GRP * SUB, TOK, DM), BF), 1)


def gx_kernel(dn_ref, x_ref, gz_ref, sc_ref, gx_ref, gs_ref, sa_ref):
    @pl.when(first_step())
    def _():
        gs_ref[...] = jnp.zeros_like(gs_ref)

    for j, cols in lane_tiles():
        sa_ref[j] = dn_ref[:, cols]

    def grad(b, j):
        return sa_ref[j, pl.ds(b, TILE, stride=SUB), :]

    rows = row_scales(x_ref, lambda b, j, cols: grad(b, j) * (1.0 + sc_ref[:, cols]))
    back = [rstd * rstd * rstd * mean for rstd, mean in rows]
    for j, cols in lane_tiles():
        scale = 1.0 + sc_ref[:, cols]
        total = gs_ref[:, cols]
        for b in range(SUB):
            xf = x_ref[b, :, cols].astype(F32)
            dn = grad(b, j) * rows[b][0]
            total = total + both(dn * xf)
            gx_ref[b, :, cols] = (gz_ref[b, :, cols].astype(F32) + (dn * scale - xf * back[b])).astype(BF)
        gs_ref[:, cols] = total


def gx_call(dn, x, gz, scale):
    return row_call(gx_kernel, 70, (dn, x, gz, scale), [ROW_BLOCK, SEQ_BLOCK, SEQ_BLOCK, ONE_ROW], [SEQ_BLOCK, SUM_BLOCK],
                    [sds((GRP * SUB, TOK, DM), BF), sds((SUB, DM), F32)], 1)


def cast_kernel(*refs):
    outs, tok = refs[-4:-1], refs[-1]
    tok[...] = jnp.zeros_like(tok)
    for which in range(2):
        @pl.when(pl.program_id(0) == which)
        def _(which=which):
            for kind in range(3):
                outs[kind][...] = refs[3 * which + kind][0].astype(BF)


def cast_call(phase, a_half, b_half, prev, after):
    def half_row(s):
        core = lax.axis_index("cp")
        return core + s * (1 - 2 * core)

    def half_spec(which, kind):
        return pl.BlockSpec((1, HALF, CH), lambda s, r: ((r * s if which else r * (1 - s) + 3 * s), kind, 0))

    in_specs = [half_spec(which, kind) for which in range(2) for kind in range(3)]
    args = [a_half] * 3 + [b_half] * 3
    alias = {}
    if prev is not None:
        alias = {len(args) + k: k for k in range(3)}
        args += list(prev)
        in_specs += [ANY] * 3
    args += list(after)
    in_specs += [ANY] * len(after)
    *weights, tok = pl.pallas_call(
        cast_kernel, grid=(2, 4), in_specs=in_specs,
        out_specs=[pl.BlockSpec((HALF, CH), lambda s, r: (half_row(s), r * 2 + phase % 2))] * 3 + [pl.BlockSpec((SUB, LANES), lambda s, r: (0, 0))],
        out_shape=[sds((DM, HALF), BF)] * 3 + [TOKEN], input_output_aliases=alias,
        compiler_params=params(), cost_estimate=cost(25))(*args)
    return weights, tok


def run(steps):
    for _ in steps:
        pass


LAG_TAPS, LAG_GATES, LAG_GRADS, LAG_BACK, LAG_DX = 4, 5, 10, 11, 15
STRIPS = tuple(range(0, PIECE, STRIP))


def rnn_kernel(own, groups, units, chip_of, col_of, *refs):
    it = iter(refs)

    def take(count):
        return [next(it) for _ in range(count)]

    n_hbm, g_hbm, wy_hbm, wx_hbm, wo_hbm = take(5)
    gate_hbm = take(1 if own else 2)
    par_ref, pos_ref = take(2)
    if own:
        outs = take(9)
        conv_hbm, dpre_hbm, stat_ref = take(3)
    else:
        take(3)
        outs = take(3)
    tok_ref, = take(1)
    nbuf, gbuf, wbuf, wgf, wgb, py, dm, xbuf, ab, uv, yb, w1b, pb, qab, qib, mib, dbuf, conv, pre, dpre, dconv, st_m, st_y, st_x, st1, st2, enter, csend, crecv = take(29)
    if own:
        rb = next(it)
    n_sem, g_sem, w_sem, wg_sem, o_sem, c_send, c_recv, d_send, d_recv, x_send, x_recv = take(11)
    if own:
        p_sem = next(it)

    core = lax.axis_index("cp")
    peer = 1 - core
    pieces = GROWS // PIECE
    steps = units * pieces
    xslots = xbuf.shape[0]
    share = 220 if own else 180

    def unit_of(q):
        return lax.div(q, pieces), lax.rem(q, pieces)

    def block_of(u):
        return lax.div(u, groups), lax.rem(u, groups)

    def al(val, mult=SUB):
        return pl.multiple_of(val, mult)

    def row_copy(q, which):
        u, i = unit_of(q)
        rows = pl.ds(al(block_of(u)[1] * GROWS + i * PIECE, PIECE), PIECE)
        slot = lax.rem(q, 2)
        src, dst, sem = ((n_hbm, nbuf, n_sem), (g_hbm, gbuf, g_sem))[which]
        return pltpu.make_async_copy(src.at[rows], dst.at[slot], sem.at[slot])

    def weight_copy(blk, which):
        slot = lax.rem(blk, 2)
        src = (wy_hbm, wx_hbm, wo_hbm)[which]
        return pltpu.make_async_copy(src.at[:, pl.ds(al(col_of(blk, False) * CH, CH), CH)], wbuf.at[slot, which], w_sem.at[slot, which])

    def gate_copies(blk):
        slot = lax.rem(blk, 2)
        chip, j = chip_of(blk)
        if own:
            return [pltpu.make_async_copy(gate_hbm[0].at[j], wgf.at[slot], wg_sem.at[0, slot])]
        rows = pl.ds(3 * HALF, CH)
        return [pltpu.make_async_copy(gate_hbm[w].at[chip, rows], wgf.at[slot, (peer if w else core)], wg_sem.at[w, slot]) for w in range(2)]

    def out_copy(q, lag, which, forward):
        u, i = unit_of(q - lag)
        blk, grp = block_of(u)
        p = i if forward is None else i + forward * (pieces - 1 - 2 * i)
        slot = lax.rem(q, 2)
        src = (st_m, st_y, st_x)[which % 3].at[slot]
        rows = pl.ds(al(grp * GROWS + p * PIECE, PIECE), PIECE)
        col = blk if which >= 6 else col_of(blk, True)
        return pltpu.make_async_copy(src, outs[which].at[rows, pl.ds(al(col * CH, CH), CH)], o_sem.at[which, slot])

    def conv_copy(q):
        u, i = unit_of(q - LAG_TAPS)
        blk, grp = block_of(u)
        p = i + core * (pieces - 1 - 2 * i)
        slot = lax.rem(q, 2)
        rows = pl.ds(al(grp * GROWS + p * PIECE, PIECE), PIECE)
        return pltpu.make_async_copy(conv.at[slot], conv_hbm.at[rows, pl.ds(al(blk * CH, CH), CH)], p_sem.at[0, slot])

    def dpre_copy(q):
        u, i = unit_of(q - LAG_GRADS)
        blk, grp = block_of(u)
        p = i + peer * (pieces - 1 - 2 * i)
        slot = lax.rem(q, 2)
        rows = pl.ds(al(grp * GROWS + p * PIECE, PIECE), PIECE)
        return pltpu.make_async_copy(dpre.at[slot], dpre_hbm.at[rows, pl.ds(al(blk * 2 * CH, CH), 2 * CH)], p_sem.at[1, slot])

    def remote(src, dst, send, recv):
        return pltpu.make_async_remote_copy(src_ref=src, dst_ref=dst, send_sem=send, recv_sem=recv, device_id={"cp": peer}, device_id_type=pl.DeviceIdType.MESH)

    def halo_copy(u):
        slot, sem = lax.rem(u, xslots), lax.rem(u, 2)
        return remote(xbuf.at[slot, pl.ds(HALO + GROWS - 24, 24)], xbuf.at[slot, pl.ds(HALO - 24, 24)], x_send.at[sem], x_recv.at[sem])

    def carry_copy(u):
        slot = lax.rem(u, 2)
        return remote(csend.at[slot], crecv.at[slot], c_send.at[slot], c_recv.at[slot])

    def dconv_copy(u):
        slot = lax.rem(u, 2)
        return remote(dbuf.at[slot, pl.ds(0, 24)], dbuf.at[slot, pl.ds(GROWS, 24)], d_send.at[slot], d_recv.at[slot])

    def out_copies(q):
        grads = (q >= LAG_GRADS) & (q < steps + LAG_GRADS)
        last = (q >= LAG_DX) & (q < steps + LAG_DX)
        made = []
        for which in range(len(outs)):
            lag, forward, when = (LAG_DX, None, last) if which % 3 == 2 else (LAG_GRADS, peer, grads)
            if own and which < 6:
                late = q - lag >= steps // 2
                when = when & (late if which >= 3 else ~late)
            made.append((when, functools.partial(out_copy, q, lag, which, forward)))
        if own:
            made += [((q >= LAG_TAPS) & (q < steps + LAG_TAPS), lambda: conv_copy(q)), (grads, lambda: dpre_copy(q))]
        return made

    def at(q, lag, i):
        return (q >= lag) & (q < steps + lag) & (lax.rem(q - lag + pieces, pieces) == i)

    def rowpos(base, k):
        pos = pos_ref[pl.ds(al(base + k * SUB), STRIP), :]
        return jnp.concatenate([pos, pos], axis=1)

    def param(blk, k):
        chip, j = chip_of(blk)
        return par_ref[chip, j, k:k + 1, :]

    def stage_at(q, lag):
        u, i = unit_of(jnp.maximum(q - lag, 0))
        blk, grp = block_of(u)
        return u, i, blk, grp

    zero = lax.div(core, 2)

    def folded(val):
        return jnp.sum(val.reshape(STRIP // SUB, SUB, CH), axis=0)

    def scan_piece(slot, p, back, state):
        first = (p * (PIECE // SUB) + back * (PIECE // SUB - 1)) * SUB
        ahead, stride = first + SUB * back, SUB - 16 * back
        for tt in range(PIECE // SUB):
            decay = ab[slot, pl.ds(al(ahead + tt * stride), SUB), :]
            at_t = pl.ds(al(first + tt * stride + SUB), SUB)
            state = uv[back, slot, at_t, :] + decay * state
            uv[back, slot, at_t, :] = state
            yield 6
        return state

    def products(q):
        u, i, blk, _ = stage_at(q, 0)
        slot, w, us, xs = lax.rem(q, 2), lax.rem(blk, 2), lax.rem(u, 2), lax.rem(u, xslots)
        totals = []
        for src, kind in ((nbuf, 1), (nbuf, 0), (gbuf, 2)):
            total = None
            for k in range(0, DM, KSTEP):
                part = jnp.dot(src[slot, :, k:k + KSTEP], wbuf[w, kind, k:k + KSTEP], preferred_element_type=F32)
                total = part if total is None else total + part
                yield
            if kind == 1:
                total = (total + param(blk, 11)).astype(BF).astype(F32)
                xbuf[xs, pl.ds(al(i * PIECE + HALO), PIECE), :] = total
            totals.append(total)
        yield
        rows = pl.ds(al(i * PIECE, PIECE), PIECE)
        py[us, rows, :] = totals[1] + param(blk, 10)
        dm[us, rows, :] = totals[2]

    def taps(q):
        u, i, blk, grp = stage_at(q, LAG_TAPS)
        base = (i + core * (pieces - 1 - 2 * i)) * PIECE
        xs, cs = lax.rem(u, xslots), lax.rem(q, 2)
        par = [param(blk, k) for k in range(5)]
        for rt in STRIPS:
            pos = rowpos(grp * POS_ROWS + base + rt, 0)
            acc = par[0]
            for k in range(4):
                xk = xbuf[xs, pl.ds(al(base + rt + HALO - SUB * k), STRIP), :]
                if k:
                    xk = jnp.where(pos >= float(k), xk, 0.0)
                acc = acc + xk * par[1 + k]
            conv[cs, rt:rt + STRIP, :] = acc.astype(BF)
            yield 34
        pre[:PIECE] = jnp.dot(conv[cs], wgb[lax.rem(blk, 2)], preferred_element_type=F32)

    def gates(q):
        u, i, blk, grp = stage_at(q, LAG_GATES)
        p = i + core * (pieces - 1 - 2 * i)
        slot, cs = lax.rem(u, 2), lax.rem(q + 1, 2)
        base = p * PIECE
        ba, bi, kh = (param(blk, k) for k in range(5, SUB))
        for rt in STRIPS:
            rd = pl.ds(al(rt + zero * STRIP, STRIP), STRIP)
            rows = pl.ds(al(base + rt, STRIP), STRIP)
            rows8 = pl.ds(al(base + rt + SUB), STRIP)
            v = py[slot, rows, :]
            dmv = dm[slot, rows, :]
            v2 = v * v
            g = 0.5 * jnp.tanh(v * (v2 * GELU_K1 + GELU_K0)) + 0.5
            y = v * g
            yb[slot, rows, :] = y
            w1b[slot, rows, :] = dmv * (g + (v * (g - g * g)) * (v2 * (6.0 * GELU_K1) + 2.0 * GELU_K0))
            uv[1, slot, rows8, :] = dmv * y
            r2 = jnp.tanh(pre[rd, :CH] + ba) + 1.0
            thi = jnp.tanh(pre[rd, CH:] + bi)
            rate = jnp.where(rowpos(grp * POS_ROWS + base + rt, 0) < 0.5, FAR, r2 * kh)
            a = jnp.exp2(rate * -LOG2E)
            msq = jnp.tanh(rate) * (1.0 + a * a)
            rs = lax.rsqrt(jnp.maximum(msq, TINY))
            c = conv[cs, rt:rt + STRIP, :].astype(F32)
            gi = 0.5 * thi + 0.5
            mi = (msq * rs) * gi
            u_in = mi * c
            ab[slot, rows, :] = a
            mib[slot, rows, :] = mi
            uv[0, slot, rows8, :] = u_in
            pb[slot, rows, :] = (gi * c) * (a * rs)
            qab[slot, rows, :] = (a * rate) * (2.0 - r2)
            qib[slot, rows, :] = u_in * (1.0 - thi)
            if own:
                rb[slot, rows, :] = a * r2
            yield 112
        state = yield from scan_piece(slot, p, core, jnp.where(i == 0, 0.0, st1[...]))
        st1[...] = state
        csend[slot] = ab[slot, pl.ds(al(peer * GROWS), SUB), :] * state

    def grads(q):
        _, i, blk, _ = stage_at(q, LAG_GRADS)
        p = i + peer * (pieces - 1 - 2 * i)
        slot = lax.rem(lax.div(q + 3 * pieces - LAG_GRADS, pieces) + 1, 2)
        so = lax.rem(q, 2)
        base = p * PIECE
        entering = enter[...]
        uv[0, slot, pl.ds(0, SUB), :] = jnp.where(core == 1, entering, 0.0)
        st2[...] = yield from scan_piece(slot, p, peer, jnp.where(i == 0, entering, st2[...]))
        sums = [jnp.zeros((SUB, CH), F32)] * 4
        for rt in STRIPS:
            rl = slice(rt, rt + STRIP)
            rows = pl.ds(al(base + rt, STRIP), STRIP)
            rows8 = pl.ds(al(base + rt + SUB), STRIP)
            hid = uv[0, slot, rows8, :]
            dh = uv[1, slot, rows8, :]
            st_m[so, rl, :] = (hid * yb[slot, rows, :]).astype(BF)
            dpy = w1b[slot, rows, :] * hid
            st_y[so, rl, :] = dpy.astype(BF)
            g1 = dh * (pb[slot, rows, :] - uv[0, slot, rows, :])
            dpa = g1 * qab[slot, rows, :]
            dpi = dh * qib[slot, rows, :]
            dconv[rl, :] = dh * mib[slot, rows, :]
            dpre[so, rl, :CH] = dpa.astype(BF)
            dpre[so, rl, CH:] = dpi.astype(BF)
            if own:
                for k, val in enumerate((dpy, dpa, dpi, g1 * rb[slot, rows, :])):
                    sums[k] = sums[k] + folded(val)
            yield 56
        if own:
            for k in range(4):
                stat_ref[blk, k * SUB:k * SUB + SUB, :] += jnp.where(q >= LAG_GRADS, sums[k], 0.0)

    def back(q):
        u, i, blk, grp = stage_at(q, LAG_BACK)
        base = (i + peer * (pieces - 1 - 2 * i)) * PIECE
        slot, so = lax.rem(u, 2), lax.rem(q + 1, 2)
        xs = lax.rem(lax.div(jnp.maximum(q, LAG_BACK - pieces) - LAG_BACK + 4 * pieces, pieces), xslots)
        val = lax.dot_general(dpre[so], wgb[lax.rem(blk, 2)], NT, preferred_element_type=F32)
        dbuf[slot, pl.ds(al(base, PIECE), PIECE), :] = dconv[...] + val
        yield 60
        if own:
            sums = [jnp.zeros((SUB, CH), F32)] * 5
            for rt in STRIPS:
                pos = rowpos(grp * POS_ROWS + base + rt, 0)
                dc = dbuf[slot, pl.ds(al(base + rt, STRIP), STRIP), :]
                sums[0] = sums[0] + folded(dc)
                for k in range(4):
                    xk = xbuf[xs, pl.ds(al(base + rt + HALO - SUB * k), STRIP), :]
                    if k:
                        xk = jnp.where(pos >= float(k), xk, 0.0)
                    sums[1 + k] = sums[1 + k] + folded(dc * xk)
                yield 40
            for k in range(5):
                stat_ref[blk, (5 + k) * SUB:(5 + k) * SUB + SUB, :] += jnp.where(q >= LAG_BACK, sums[k], 0.0)

    def taps_back(q):
        u, i, blk, grp = stage_at(q, LAG_DX)
        slot, so = lax.rem(u, 2), lax.rem(q, 2)
        base = i * PIECE
        par = [param(blk, k) for k in range(1, 5)]
        total = jnp.zeros((SUB, CH), F32)
        for rt in STRIPS:
            acc = dbuf[slot, pl.ds(al(base + rt), STRIP), :] * par[0]
            for k in range(1, 4):
                dk = dbuf[slot, pl.ds(al(base + rt + SUB * k), STRIP), :]
                acc = acc + jnp.where(rowpos(grp * POS_ROWS + base + rt, k) >= float(k), dk, 0.0) * par[k]
            st_x[so, rt:rt + STRIP, :] = acc.astype(BF)
            if own:
                total = total + folded(acc)
            yield 32
        if own:
            stat_ref[blk, 32:40, :] += jnp.where(q >= LAG_DX, total, 0.0)

    def start_of_step(q):
        for when, make in out_copies(q - 2):
            @pl.when(when)
            def _(make=make):
                make().wait()

        @pl.when(at(q, LAG_TAPS, 3) & (core == 0))
        def _():
            halo_copy(lax.div(q - LAG_TAPS, pieces)).wait_send()

        @pl.when(at(q, LAG_TAPS, 3) & (core == 1))
        def _():
            halo_copy(lax.div(q - LAG_TAPS, pieces)).wait_recv()

        @pl.when(at(q, LAG_GRADS, 0))
        def _():
            u = lax.div(q - LAG_GRADS, pieces)
            carry_copy(u).wait()
            enter[...] = crecv[lax.rem(u, 2)]

        @pl.when(at(q, LAG_DX, 3))
        def _():
            dconv_copy(lax.div(q - LAG_DX, pieces)).wait()

        @pl.when((q >= LAG_TAPS) & (q < steps + LAG_TAPS) & (lax.rem(q - LAG_TAPS + groups * pieces, groups * pieces) == 0))
        def _():
            blk = lax.div(q - LAG_TAPS, groups * pieces)
            for cp in gate_copies(blk):
                cp.wait()
            slot = lax.rem(blk, 2)
            wgb[slot, :, :CH] = wgf[slot, 0].astype(BF)
            wgb[slot, :, CH:] = wgf[slot, 1].astype(BF)

            @pl.when(blk + 1 < units // groups)
            def _():
                for cp in gate_copies(blk + 1):
                    cp.start()

    def end_of_step(q):
        for when, make in out_copies(q):
            @pl.when(when)
            def _(make=make):
                make().start()

        @pl.when(at(q, LAG_TAPS, 0) & (core == 0))
        def _():
            halo_copy(lax.div(q - LAG_TAPS, pieces)).start()

        @pl.when(at(q, LAG_GATES, 3))
        def _():
            carry_copy(lax.div(q - LAG_GATES, pieces)).start()

        @pl.when(at(q, LAG_BACK, 3))
        def _():
            dconv_copy(lax.div(q - LAG_BACK, pieces)).start()

    for which in range(2):
        row_copy(0, which).start()
    for which in range(3):
        weight_copy(0, which).start()
    for cp in gate_copies(0):
        cp.start()
    tok_ref[...] = jnp.zeros_like(tok_ref)
    for slot in range(2):
        ab[slot, pl.ds(GROWS, SUB), :] = jnp.ones((SUB, CH), F32)
    if own:
        stat_ref[...] = jnp.zeros_like(stat_ref)
    barrier = pltpu.get_barrier_semaphore()
    pl.semaphore_signal(barrier, inc=1, device_id={"cp": peer}, device_id_type=pl.DeviceIdType.MESH)
    pl.semaphore_wait(barrier, 1)

    def full_step(q, _):
        for which in range(2):
            row_copy(q, which).wait()

        @pl.when(q + 1 < steps)
        def _():
            for which in range(2):
                row_copy(q + 1, which).start()

        @pl.when(lax.rem(q, groups * pieces) == 0)
        def _():
            blk = lax.div(q, groups * pieces)
            for which in range(3):
                weight_copy(blk, which).wait()

            @pl.when(blk + 1 < units // groups)
            def _():
                for which in range(3):
                    weight_copy(blk + 1, which).start()

        start_of_step(q)
        product_steps, spent, made = products(q), share, 0
        for stage in (taps_back, back, grads, gates, taps):
            for bundles in stage(q):
                spent += bundles
                while spent >= share and made < 3 * DM // KSTEP:
                    spent -= share
                    made += 1
                    next(product_steps)
        run(product_steps)
        end_of_step(q)
        return 0

    lax.fori_loop(0, steps, full_step, 0)

    def drain_step(q, _):
        start_of_step(q)
        for lag, stage in ((LAG_DX, taps_back), (LAG_BACK, back), (LAG_GRADS, grads), (LAG_GATES, gates), (LAG_TAPS, taps)):
            @pl.when(q < steps + lag)
            def _(stage=stage):
                run(stage(q))
        end_of_step(q)
        return 0

    lax.fori_loop(steps, steps + LAG_DX, drain_step, 0)
    for q in (steps + LAG_DX, steps + LAG_DX + 1):
        for when, make in out_copies(jnp.int32(q - 2)):
            @pl.when(when)
            def _(make=make):
                make().wait()


def rnn_call(phase, groups, n, gz, weights, gate_src, par, pos, acts):
    own = phase is None
    units = (4 if own else 3) * groups

    def chip_of(blk):
        return (0, blk) if own else (lax.rem(lax.axis_index("tp") + 1 + blk, 4), 0)

    def col_of(blk, merged):
        if own:
            return lax.axis_index("tp") * 2 + lax.rem(blk, 2) if merged else blk
        return chip_of(blk)[0] * 2 + phase % 2

    args = [n, gz, *weights, *gate_src, par, pos, *acts]
    in_specs = [ANY] * (5 + len(gate_src)) + [VM] * 2 + [ANY] * len(acts)
    out_specs = [ANY] * 3
    out_shape = [sds((ROWS, HALF), BF)] * 3
    alias = {9 + k: k for k in range(len(acts))}
    if own:
        out_specs = [ANY] * 11 + [VM]
        out_shape = out_shape * 2 + [sds((ROWS, 4 * CH), BF)] * 4 + [sds((ROWS, SUB * CH), BF), sds((4, 80, CH), F32)]
    out_specs = out_specs + [VM]
    out_shape = out_shape + [TOKEN]

    def buf(slots, rows, dtype=F32, cols=CH):
        return pltpu.VMEM((slots, rows, cols), dtype)

    piece32 = pltpu.VMEM((PIECE, CH), F32)
    scratch = [buf(2, PIECE, BF, DM), buf(2, PIECE, BF, DM), pltpu.VMEM((2, 3, DM, CH), BF), pltpu.VMEM((2, 2, CH, CH), F32), buf(2, CH, BF, 2 * CH),
               buf(2, GROWS), buf(2, GROWS), buf(4 if own else 2, GROWS + HALO), buf(2, GROWS + SUB),
               pltpu.VMEM((2, 2, GROWS + SUB, CH), F32)] + [buf(2, GROWS)] * 6 + [buf(2, GROWS + HALO), buf(2, PIECE, BF),
               pltpu.VMEM((PIECE + STRIP, 2 * CH), F32), buf(2, PIECE, BF, 2 * CH), piece32] + [buf(2, PIECE, BF)] * 3 + [pltpu.VMEM((SUB, CH), F32)] * 3 + [buf(2, SUB)] * 2
    dma = pltpu.SemaphoreType.DMA
    sems = [dma((2,)), dma((2,)), dma((2, 3)), dma((2, 2)), dma((9 if own else 3, 2))] + [dma((2,))] * 6
    if own:
        scratch.append(buf(2, GROWS))
        sems.append(dma((2, 2)))
    return pl.pallas_call(
        functools.partial(rnn_kernel, own, groups, units, chip_of, col_of), in_specs=in_specs, out_specs=out_specs, out_shape=out_shape,
        scratch_shapes=scratch + sems, input_output_aliases=alias,
        compiler_params=params(collective_id=0 if own else 1 + phase, has_side_effects=True),
        cost_estimate=cost(10 * units))(*args)


def layer(x_in, grad_z, seg_pos, norm_scale, w_x, b_x, w_y, b_y, conv_w, conv_b, w_a, b_a, w_i, b_i, a_param, w_out, b_out):
    core = lax.axis_index("cp")
    swap = [(0, 1), (1, 0)]
    half = core * HALF

    zero = jnp.zeros_like(a_param)
    rows = [conv_b.astype(F32)] + [conv_w[k].astype(F32) for k in range(4)] + [0.5 * b_a.astype(F32), 0.5 * b_i.astype(F32), 4.0 * jax.nn.softplus(a_param), zero, zero,
            b_y.astype(F32), b_x.astype(F32)] + [zero] * 4
    par_own = jnp.stack(rows).reshape(16, 4, CH).transpose(1, 0, 2)
    wg_own = jnp.stack([w_a, w_i], axis=1).astype(F32) * 0.5
    wg_mine = lax.dynamic_index_in_dim(wg_own, core, 1, keepdims=False)

    got = []
    for j in range(4):
        cols = j * CH
        parts = [lax.dynamic_slice(w_y, (half, cols), (HALF, CH)).astype(F32), lax.dynamic_slice(w_x, (half, cols), (HALF, CH)).astype(F32),
                 lax.dynamic_slice(w_out, (cols, half), (CH, HALF)).T.astype(F32), wg_mine[j], par_own[j]]
        mine = lax.optimization_barrier(jnp.concatenate(parts, axis=0))
        got.append(lax.all_gather(mine, "tp"))

    def partner(val):
        return lax.ppermute(val, "cp", swap)

    pos = seg_pos.astype(jnp.int32)
    later = jnp.where(core == 0, partner(pos[:, :SUB]), -1)
    pos = jnp.concatenate([pos, later], axis=1).reshape(GRP, SUB, TOK + SUB).transpose(0, 2, 1).astype(F32)
    pos = jnp.broadcast_to(pos.reshape(GRP * POS_ROWS, 1), (GRP * POS_ROWS, LANES))

    scale = norm_scale.astype(F32)[None]
    n, gz, gb = norm_call(x_in, grad_z, scale)

    first = rnn_call(None, GRP, n, gz, (w_y, w_x, w_out.T), (wg_own,), par_own[None], pos, ())
    sets, (omixed, ody, odx, conv16, dpre16, stats) = [first[:3], first[3:6]], first[6:12]
    weights = [None, None]

    def dot(lhs, rhs, dims):
        return lax.dot_general(lhs, rhs, dims, preferred_element_type=F32)

    def phase(j, deps):
        s = j // 2
        other = partner(got[j])
        weights[s], _ = cast_call(j, got[j], other, weights[s], deps)
        par = got[j][:, None, 3 * HALF + CH:]
        *acts, token = rnn_call(j, GRP, n, gz, weights[s], (got[j], other), par, pos, sets[s])
        sets[s] = acts
        return token

    g_w_x = dot(n, odx, TN)
    g_w_y = dot(n, ody, TN)
    phase(0, (g_w_x, g_w_y))
    g_w_out = dot(omixed, gz, TN)
    g_gate = 0.5 * jnp.einsum("rhk,rhj->hkj", conv16.reshape(ROWS, 4, CH), dpre16.reshape(ROWS, 4, 2 * CH), preferred_element_type=F32)
    stats = jnp.sum(stats.reshape(4, 10, SUB, CH), axis=2).transpose(1, 0, 2).reshape(10, 4 * CH)
    phase(1, (g_w_out, g_gate))
    g_w_x, g_w_y, g_w_out, g_gate = lax.psum((g_w_x, g_w_y, g_w_out, g_gate), "cp")
    z_acc = dot(sets[0][0], weights[0][2], NT)
    dn = dot(sets[0][1], weights[0][0], NT)
    dn = dot(sets[0][2], weights[0][1], NT) + dn
    phase(2, (z_acc, dn))
    phase(3, ())
    z_acc = dot(sets[1][0], weights[1][2], NT) + z_acc
    z_out = z_call(z_acc, x_in, b_out.astype(F32)[None])
    dn = dot(sets[1][1], weights[1][0], NT) + dn
    dn = dot(sets[1][2], weights[1][1], NT) + dn
    grad_x, gs = gx_call(dn, x_in, grad_z, scale)

    g_scale, stats, g_b_out = lax.psum((jnp.sum(gs, axis=0), stats, jnp.sum(gb, axis=0)), "cp")
    return (z_out, grad_x, g_scale, g_w_x, stats[4], g_w_y, stats[0], stats[6:10], stats[5], g_gate[:, :, :CH], 0.5 * stats[1],
            g_gate[:, :, CH:], 0.5 * stats[2], 4.0 * jax.nn.sigmoid(a_param) * stats[3], g_w_out, g_b_out)


def solution(mesh):
    return jax.shard_map(layer, mesh=mesh, in_specs=IN_SPECS, out_specs=OUT_SPECS, check_vma=False)
```

time: 4870 us -> 2410 us (0.49)
  waiting for transfers between devices: 2030 us -> 489 us
  local copies, waits for them, and re-layouts: 1470 us -> 74.8 us
  Pallas kernels: 0 us -> 1150 us
  other arithmetic: 813 us -> 24.8 us
  matrix products: 488 us -> 649 us
    psum x4 -> x2, waiting for transfers between devices: 2030 us -> 14.5 us  [the longest x1 14.5 us: layer(): lax.psum((g_w_x, g_w_y, g_w_out, g_gate), 'cp')]
    pallas_call x0 -> x12, Pallas kernels: none -> 1150 us  [the longest x5 839 us: rnn_call(): pl.pallas_call(functools.partial(rnn_kernel, own, groups, units, chip_of,...]
    dynamic_update_slice x516 -> x0, local copies, waits for them, and re-layouts: 979 us -> none  [the longest x512 977 us: local_scan(): lax.scan(scan_step, (zeros_h, jnp.ones_like(zeros_h)), (decays, drives))]
    all_gather x0 -> x4, waiting for transfers between devices: none -> 473 us  [layer(): got.append(lax.all_gather(mine, 'tp'))]
    dynamic_slice x257 -> x0, local copies, waits for them, and re-layouts: 338 us -> none  [the longest x256 338 us: local_scan(): lax.scan(scan_step, (zeros_h, jnp.ones_like(zeros_h)), (decays, drives))]
    reduce_sum x10 -> x3, other arithmetic: 318 us -> 3.17 us  [the longest x1 1.54 us: layer(): jnp.sum(gs, axis=0)]
    dynamic_update_slice x130 -> x0, other arithmetic: 223 us -> none  [the longest x128 223 us: local_scan(): lax.scan(scan_step, (zeros_h, jnp.ones_like(zeros_h)), (decays, drives))]
    dot_general x15 -> x10, matrix products: 488 us -> 649 us  [the longest x9 635 us: dot(): return lax.dot_general(lhs, rhs, dims, preferred_element_type=F32)]
  transfers between devices with their start and end apart: 6 -> 11, of which waited for: 4 -> 4; matrix products, arithmetic and copies ran while one was open for 11% -> 21% of each run, Pallas kernels for 0% -> 37%
where the time goes in v1:
time: 2410 us; the launch traced here: 2400 us
  Pallas kernels  1150 us (48%)
  matrix products  649 us (27%)
  waiting for transfers between devices  489 us (20%)
  local copies, waits for them, and re-layouts  74.8 us (3%)
  other arithmetic  24.8 us (1%)
    pallas_call x5, Pallas kernels, rnn_call(): pl.pallas_call(functools.partial(rnn_kernel, own, groups, units, chip_of,...  839 us
    dot_general x9, matrix products, dot(): return lax.dot_general(lhs, rhs, dims, preferred_element_type=F32)  635 us
    all_gather x4, waiting for transfers between devices, layer(): got.append(lax.all_gather(mine, 'tp'))  473 us
    pallas_call x3, Pallas kernels, row_call(): pl.pallas_call(kernel, grid=(GRP, NTOK), in_specs=in_specs, out_specs=out...  203 us
    pallas_call x4, Pallas kernels, cast_call(): pl.pallas_call(cast_kernel, grid=(2, 4), in_specs=in_specs, out_specs=[pl...  107 us
    unnamed x53, local copies, waits for them, and re-layouts  49.4 us
  transfers between devices with their start and end apart: 11, of which 4 were waited for; matrix products, arithmetic and copies ran while one was open for 21% of the time, Pallas kernels for 37%

profile of v1, /device:TPU:0, one launch (start us, length us, event | category | flops | bytes accessed | tf_op | source)
XLA Modules:
  0.0 2403.0 jit_solution(2508095080483334673)
XLA Ops:
  7.3 12.0 copy.106
  25.4 6.5 convert_dynamic-update-slice_fusion.4
  42.5 65.6 %shard_map.288 = (bf16[4096,4096]{1,0:T(8,128)(2,1)}, bf16[4096,4096]{1,0:T(8,128)(2,1)}, f32[8,4096]{1,0:T(8,128)}) custom-call(bf16[32,128,4096]{2,1,0:T(8,128)(2,1)} %x_ref.5, bf16[32,128,4096]{2,1,0:T(8,128)(2,1)} %gz_ref.3, f32[1,4096]{1,0:T(1,128)} %bitcast.159), custom_call_target="tpu_custom_call" | custom-call | flops 60000002048 | bytes 60000000 | tf_op jit(solution)/shard_map/pallas_call | solution.py:63
  110.0 163.5 %all-gather.15.cloned.1.call-done = f32[25664,256]{1,0:T(8,128)} async-done(((f32[6416,256]{1,0:T(8,128)}), f32[25664,256]{1,0:T(8,128)}) %all-gather.15.cloned.1.call-update) | async-done | bytes 26279952 | tf_op jit(solution)/shard_map/all_gather | solution.py:679
  275.6 225.7 %shard_map.289 = (bf16[4096,2048]{1,0:T(8,128)(2,1)}, bf16[4096,2048]{1,0:T(8,128)(2,1)}, bf16[4096,2048]{1,0:T(8,128)(2,1)}, bf16[4096,2048]{1,0:T(8,128)(2,1)}...) custom-call(bf16[4096,4096]{1,0:T(8,128)(2,1)} %get-tuple-element.57, ...), custom_call_target="tpu_custom_call" | custom-call | flops 160000000000 | bytes 160000000 | tf_op jit(solution)/shard_map/pallas_call | solution.py:654
  501.3 12.0 copy.115
  514.0 47.8 %fusion.15.refs_6_ = f32[4096,1024]{1,0:T(8,128)} fusion(bf16[4096,4096]{1,0:T(8,128)(2,1)} %get-tuple-element.57.refs_0_, bf16[4096,1024]{1,0:T(8,128)(2,1)} %get-tuple-element.59), kind=kOutput, calls=%fused_computation.54 | convolution fusion | flops 34359738368 | bytes 58720256 | tf_op jit(solution)/shard_map/dot_general | solution.py:697
  562.2 14.0 fusion.3.refs_10_
  576.2 43.7 %fusion.17.refs_9_ = f32[1024,4096]{1,0:T(8,128)} fusion(bf16[4096,1024]{1,0:T(8,128)(2,1)} %get-tuple-element.64, bf16[4096,4096]{1,0:T(8,128)(2,1)} %get-tuple-element.58.refs_1_), kind=kOutput, calls=%fused_computation.56 | convolution fusion | flops 34359738368 | bytes 58720256 | tf_op jit(solution)/shard_map/dot_general | solution.py:697
  619.9 43.8 %fusion.16.refs_7_ = f32[4096,1024]{1,0:T(8,128)} fusion(bf16[4096,4096]{1,0:T(8,128)(2,1)} %get-tuple-element.57.refs_0_, bf16[4096,1024]{1,0:T(8,128)(2,1)} %get-tuple-element.60), kind=kOutput, calls=%fused_computation.55 | convolution fusion | flops 34359738368 | bytes 58720256 | tf_op jit(solution)/shard_map/dot_general | solution.py:697
  663.6 76.5 %all-gather.11.cloned.1.call-done = f32[25664,256]{1,0:T(8,128)} async-done(((f32[6416,256]{1,0:T(8,128)}), f32[25664,256]{1,0:T(8,128)}) %all-gather.11.cloned.1.call-update) | async-done | bytes 26279952 | tf_op jit(solution)/shard_map/all_gather | solution.py:679
  740.2 232.9 %all-gather.9.cloned.1.call-done = f32[25664,256]{1,0:T(8,128)} async-done(((f32[6416,256]{1,0:T(8,128)}), f32[25664,256]{1,0:T(8,128)}) %all-gather.9.cloned.1.call-update) | async-done | bytes 26279952 | tf_op jit(solution)/shard_map/all_gather | solution.py:679
  979.0 26.7 %shard_map.290 = (bf16[4096,2048]{1,0:T(8,128)(2,1)}, bf16[4096,2048]{1,0:T(8,128)(2,1)}, bf16[4096,2048]{1,0:T(8,128)(2,1)}, f32[8,128]{1,0:T(8,128)}) custom-call(f32[4,6416,256]{2,1,0:T(8,128)} %bitcast.130, f32[4,6416,256]{2,1,0:T(8,128)} %bitcast.131, f32[4,6416,256]{2,1,0:T(8,128)} %bitcast.132, ...), custom_call_target="tpu_custom_call" | custom-call | flops 24999999488 | bytes 25000000 | tf_op jit(solution)/shard_map/pallas_call | solution.py:181
  1005.6 153.9 %shard_map.292 = (bf16[4096,2048]{1,0:T(8,128)(2,1)}, bf16[4096,2048]{1,0:T(8,128)(2,1)}, bf16[4096,2048]{1,0:T(8,128)(2,1)}, f32[8,128]{1,0:T(8,128)}) custom-call(bf16[4096,4096]{1,0:T(8,128)(2,1)} %get-tuple-element.57.refs_0_, bf16[4096,4096]{1,0:T(8,128)(2,1)} %get-tuple-element.58.refs_1_, ...), custom_call_target="tpu_custom_call", output_to_operand_aliasing={{0}: (9, {}), {1}: (10, {}), {2}: (11, {})} | custom-call | flops 120000004096 | bytes 120000000 | tf_op jit(solution)/shard_map/pallas_call | solution.py:654
  1159.6 26.6 %shard_map.291 = (bf16[4096,2048]{1,0:T(8,128)(2,1)}, bf16[4096,2048]{1,0:T(8,128)(2,1)}, bf16[4096,2048]{1,0:T(8,128)(2,1)}, f32[8,128]{1,0:T(8,128)}) custom-call(f32[4,6416,256]{2,1,0:T(8,128)} %bitcast.136, f32[4,6416,256]{2,1,0:T(8,128)} %bitcast.137, f32[4,6416,256]{2,1,0:T(8,128)} %bitcast.138, ...), custom_call_target="tpu_custom_call", output_to_operand_aliasing={{0}: (6, {}), {1}: (7, {}), {2}: (8, {})} | custom-call | flops 24999999488 | bytes 25000000 | tf_op jit(solution)/shard_map/pallas_call | solution.py:181
  1186.2 153.3 %shard_map.293 = (bf16[4096,2048]{1,0:T(8,128)(2,1)}, bf16[4096,2048]{1,0:T(8,128)(2,1)}, bf16[4096,2048]{1,0:T(8,128)(2,1)}, f32[8,128]{1,0:T(8,128)}) custom-call(bf16[4096,4096]{1,0:T(8,128)(2,1)} %get-tuple-element.57.refs_0_, bf16[4096,4096]{1,0:T(8,128)(2,1)} %get-tuple-element.58.refs_1_, ...), custom_call_target="tpu_custom_call", output_to_operand_aliasing={{0}: (9, {}), {1}: (10, {}), {2}: (11, {})} | custom-call | flops 120000004096 | bytes 120000000 | tf_op jit(solution)/shard_map/pallas_call | solution.py:654
  1339.5 78.8 %fusion.19 = f32[4096,4096]{1,0:T(8,128)} fusion(bf16[4096,2048]{1,0:T(8,128)(2,1)} %get-tuple-element.78, bf16[4096,2048]{1,0:T(8,128)(2,1)} %get-tuple-element.67.refs_2_), kind=kOutput, calls=%fused_computation.58 | convolution fusion | flops 68719476736 | bytes 100663296 | tf_op jit(solution)/shard_map/dot_general | solution.py:697
  1418.3 83.9 %convolution_add_fusion.1.refs_7_ = f32[4096,4096]{1,0:T(8,128)} fusion(f32[4096,4096]{1,0:T(8,128)} %fusion.19, bf16[4096,2048]{1,0:T(8,128)(2,1)} %get-tuple-element.77, bf16[4096,2048]{1,0:T(8,128)(2,1)} %get-tuple-element.68.refs_3_), kind=kOutput, calls=%fused_computation.2 | convolution fusion | flops 68736253952 | bytes 167772160 | tf_op jit(solution)/shard_map/dot_general | solution.py:697
  1502.2 79.0 %fusion.18.refs_6_ = f32[4096,4096]{1,0:T(8,128)} fusion(bf16[4096,2048]{1,0:T(8,128)(2,1)} %get-tuple-element.76, bf16[4096,2048]{1,0:T(8,128)(2,1)} %get-tuple-element.69.refs_4_), kind=kOutput, calls=%fused_computation.57 | convolution fusion | flops 68719476736 | bytes 100663296 | tf_op jit(solution)/shard_map/dot_general | solution.py:697
  1581.1 26.7 %shard_map.294 = (bf16[4096,2048]{1,0:T(8,128)(2,1)}, bf16[4096,2048]{1,0:T(8,128)(2,1)}, bf16[4096,2048]{1,0:T(8,128)(2,1)}, f32[8,128]{1,0:T(8,128)}) custom-call(f32[4,6416,256]{2,1,0:T(8,128)} %bitcast.124, f32[4,6416,256]{2,1,0:T(8,128)} %bitcast.125, f32[4,6416,256]{2,1,0:T(8,128)} %bitcast.126, ...), custom_call_target="tpu_custom_call" | custom-call | flops 24999999488 | bytes 25000000 | tf_op jit(solution)/shard_map/pallas_call | solution.py:181
  1607.8 153.3 %shard_map.296 = (bf16[4096,2048]{1,0:T(8,128)(2,1)}, bf16[4096,2048]{1,0:T(8,128)(2,1)}, bf16[4096,2048]{1,0:T(8,128)(2,1)}, f32[8,128]{1,0:T(8,128)}) custom-call(bf16[4096,4096]{1,0:T(8,128)(2,1)} %get-tuple-element.57.refs_0_, bf16[4096,4096]{1,0:T(8,128)(2,1)} %get-tuple-element.58.refs_1_, ...), custom_call_target="tpu_custom_call", output_to_operand_aliasing={{0}: (9, {}), {1}: (10, {}), {2}: (11, {})} | custom-call | flops 120000004096 | bytes 120000000 | tf_op jit(solution)/shard_map/pallas_call | solution.py:654
  1761.1 27.1 %shard_map.295 = (bf16[4096,2048]{1,0:T(8,128)(2,1)}, bf16[4096,2048]{1,0:T(8,128)(2,1)}, bf16[4096,2048]{1,0:T(8,128)(2,1)}, f32[8,128]{1,0:T(8,128)}) custom-call(f32[4,6416,256]{2,1,0:T(8,128)} %bitcast.118, f32[4,6416,256]{2,1,0:T(8,128)} %bitcast.119, f32[4,6416,256]{2,1,0:T(8,128)} %bitcast.120, ...), custom_call_target="tpu_custom_call", output_to_operand_aliasing={{0}: (6, {}), {1}: (7, {}), {2}: (8, {})} | custom-call | flops 24999999488 | bytes 25000000 | tf_op jit(solution)/shard_map/pallas_call | solution.py:181
  1788.2 153.3 %shard_map.297 = (bf16[4096,2048]{1,0:T(8,128)(2,1)}, bf16[4096,2048]{1,0:T(8,128)(2,1)}, bf16[4096,2048]{1,0:T(8,128)(2,1)}, f32[8,128]{1,0:T(8,128)}) custom-call(bf16[4096,4096]{1,0:T(8,128)(2,1)} %get-tuple-element.57.refs_0_, bf16[4096,4096]{1,0:T(8,128)(2,1)} %get-tuple-element.58.refs_1_, ...), custom_call_target="tpu_custom_call", output_to_operand_aliasing={{0}: (9, {}), {1}: (10, {}), {2}: (11, {})} | custom-call | flops 120000004096 | bytes 120000000 | tf_op jit(solution)/shard_map/pallas_call | solution.py:654
  1941.5 78.8 %fusion.20 = f32[4096,4096]{1,0:T(8,128)} fusion(bf16[4096,2048]{1,0:T(8,128)(2,1)} %get-tuple-element.93, bf16[4096,2048]{1,0:T(8,128)(2,1)} %get-tuple-element.82.refs_2_), kind=kOutput, calls=%fused_computation.59 | convolution fusion | flops 68719476736 | bytes 100663296 | tf_op jit(solution)/shard_map/dot_general | solution.py:697
  2020.3 94.4 %add_add_fusion.dn_ref = f32[4096,4096]{1,0:T(8,128)} fusion(f32[4096,4096]{1,0:T(8,128)} %fusion.20, f32[4096,4096]{1,0:T(8,128)} %convolution_add_fusion.1.refs_7_, bf16[4096,2048]{1,0:T(8,128)(2,1)} %get-tuple-element.92, bf16[4096,2048]{1,0:T(8,128)(2,1)} %get-tuple-element.83.refs_3_), kind=kOutput, calls=%fused_computation | convolution fusion | flops 68753031168 | bytes 234881024 | tf_op jit(solution)/shard_map/dot_general | solution.py:697
  2114.7 73.6 %shard_map.299 = (bf16[32,128,4096]{2,1,0:T(8,128)(2,1)}, f32[8,4096]{1,0:T(8,128)}) custom-call(f32[4096,4096]{1,0:T(8,128)} %add_add_fusion.dn_ref, bf16[32,128,4096]{2,1,0:T(8,128)(2,1)} %x_ref.5, bf16[32,128,4096]{2,1,0:T(8,128)(2,1)} %gz_ref.3, f32[1,4096]{1,0:T(1,128)} %bitcast.160), custom_call_target="tpu_custom_call" | custom-call | flops 70000001024 | bytes 70000000 | tf_op jit(solution)/shard_map/pallas_call | solution.py:63
  2191.2 84.6 %convolution_add_fusion.acc_ref = f32[4096,4096]{1,0:T(8,128)} fusion(f32[4096,4096]{1,0:T(8,128)} %fusion.18.refs_6_, bf16[4096,2048]{1,0:T(8,128)(2,1)} %get-tuple-element.91, bf16[4096,2048]{1,0:T(8,128)(2,1)} %get-tuple-element.84.refs_4_), kind=kOutput, calls=%fused_computation.1 | convolution fusion | flops 68736253952 | bytes 167772160 | tf_op jit(solution)/shard_map/dot_general | solution.py:697
  2275.8 63.3 %shard_map.298 = bf16[32,128,4096]{2,1,0:T(8,128)(2,1)} custom-call(f32[4096,4096]{1,0:T(8,128)} %convolution_add_fusion.acc_ref, bf16[32,128,4096]{2,1,0:T(8,128)(2,1)} %x_ref.5, f32[1,4096]{1,0:T(1,128)} %bitcast.161), custom_call_target="tpu_custom_call" | custom-call | flops 49999998976 | bytes 50000000 | tf_op jit(solution)/shard_map/pallas_call | solution.py:63
  2342.8 14.5 all-reduce.7.cloned.1.call-done
  2361.6 13.7 copy.166
  2378.0 8.5 copy.167
  2389.1 6.2 copy.168
  (107 shorter events, 44.2 us)
Async XLA Ops:
  7.2 12.2 copy-start.13
  7.2 12.2 copy-start.6
  7.2 12.2 copy-start.14
  7.2 12.2 copy-start.15
  7.2 12.2 copy-start.7
  7.2 12.2 copy-start.16
  7.2 12.2 copy-start.17
  7.3 18.0 copy-start.2
  7.3 18.0 copy-start.3
  7.3 266.3 %all-gather.15.cloned.1.call-start = ((), (), s32[]{:S(2)}) async-start(), calls=%async_computation.3 | async-start | bytes 32849920 | tf_op jit(solution)/shard_map/all_gather | solution.py:679
  25.4 14.0 copy-start.1
  31.9 9.1 copy-start.10
  37.7 4.3 copy-start.11
  38.8 0.8 copy-start.5
  39.5 522.4 %all-gather.13.cloned.1.call-start = ((), (), s32[]{:S(2)}) async-start(), calls=%async_computation.2 | async-start | bytes 32849920 | tf_op jit(solution)/shard_map/all_gather | solution.py:679
  40.2 700.0 %all-gather.11.cloned.1.call-start = ((), (), s32[]{:S(2)}) async-start(), calls=%async_computation.1 | async-start | bytes 32849920 | tf_op jit(solution)/shard_map/all_gather | solution.py:679
  40.9 932.1 %all-gather.9.cloned.1.call-start = ((), (), s32[]{:S(2)}) async-start(), calls=%async_computation | async-start | bytes 32849920 | tf_op jit(solution)/shard_map/all_gather | solution.py:679
  41.0 68.7 %collective-permute-start.4 = (s32[32,8]{1,0:T(8,128)S(1)}, s32[32,8]{1,0:T(8,128)S(1)}, u32[]{:S(2)}, u32[]{:S(2)}) collective-permute-start(s32[32,8]{1,0:T(8,128)S(1)} %bitcast.162), channel_id=1, source_target_pairs={{0,1},{1,0},{2,3},{3,2},{4,5},{5,4},{6,7},{7,6}} | collective-permute-start | bytes 3080 | tf_op jit(solution)/shard_map/ppermute | solution.py:682
  41.9 2297.2 %all-reduce.5.cloned.1.call-start = ((), (), s32[]{:S(2)}) async-start(), calls=%async_computation.4 | async-start | bytes 196608 | tf_op jit(solution)/shard_map/psum | solution.py:727
  273.6 705.4 %collective-permute-start.3 = (f32[4,6416,256]{2,1,0:T(8,128)}, f32[4,6416,256]{2,1,0:T(8,128)}, u32[]{:S(2)}, u32[]{:S(2)}) collective-permute-start(f32[4,6416,256]{2,1,0:T(8,128)} %bitcast.128), channel_id=1, source_target_pairs={{0,1},{1,0},{2,3},{3,2},{4,5},{5,4},{6,7},{7,6}} | collective-permute-start | bytes 78839816 | tf_op jit(solution)/shard_map/ppermute | solution.py:682
  501.3 12.0 copy-start.4
  561.8 597.7 %collective-permute-start.2 = (f32[4,6416,256]{2,1,0:T(8,128)}, f32[4,6416,256]{2,1,0:T(8,128)}, u32[]{:S(2)}, u32[]{:S(2)}) collective-permute-start(f32[4,6416,256]{2,1,0:T(8,128)} %bitcast.134), channel_id=1, source_target_pairs={{0,1},{1,0},{2,3},{3,2},{4,5},{5,4},{6,7},{7,6}} | collective-permute-start | bytes 78839816 | tf_op jit(solution)/shard_map/ppermute | solution.py:682
  740.2 840.9 %collective-permute-start.1 = (f32[4,6416,256]{2,1,0:T(8,128)}, f32[4,6416,256]{2,1,0:T(8,128)}, u32[]{:S(2)}, u32[]{:S(2)}) collective-permute-start(f32[4,6416,256]{2,1,0:T(8,128)} %bitcast.122), channel_id=1, source_target_pairs={{0,1},{1,0},{2,3},{3,2},{4,5},{5,4},{6,7},{7,6}} | collective-permute-start | bytes 78839816 | tf_op jit(solution)/shard_map/ppermute | solution.py:682
  973.1 788.0 %collective-permute-start = (f32[4,6416,256]{2,1,0:T(8,128)}, f32[4,6416,256]{2,1,0:T(8,128)}, u32[]{:S(2)}, u32[]{:S(2)}) collective-permute-start(f32[4,6416,256]{2,1,0:T(8,128)} %bitcast.116), channel_id=1, source_target_pairs={{0,1},{1,0},{2,3},{3,2},{4,5},{5,4},{6,7},{7,6}} | collective-permute-start | bytes 78839816 | tf_op jit(solution)/shard_map/ppermute | solution.py:682
  2189.9 167.4 %all-reduce.7.cloned.1.call-start = ((), (), s32[]{:S(2)}) async-start(), calls=%async_computation.5 | async-start | bytes 104857600 | tf_op jit(solution)/shard_map/psum | solution.py:715
  2275.8 66.4 %copy-start.8 = (f32[1024]{0:T(1024)S(1)}, f32[1024]{0:T(1024)}, u32[]{:S(2)}) copy-start(f32[1024]{0:T(1024)} %param.31) | copy-start | bytes 12292
  2361.6 16.4 copy-start
  2361.6 24.9 %slice-start = ((s8[16777216]{0:T(1024)(128)(4,1)}), s8[4194304]{0:T(1024)(128)(4,1)S(1)}, s32[]{:S(2)}) async-start(s8[16777216]{0:T(1024)(128)(4,1)} %bitcast.141), calls=%async_computation.6 | async-start | bytes 8388608
  2361.6 24.9 %slice-start.1 = ((s8[16777216]{0:T(1024)(128)(4,1)}), s8[4194304]{0:T(1024)(128)(4,1)S(1)}, s32[]{:S(2)}) async-start(s8[16777216]{0:T(1024)(128)(4,1)} %bitcast.141), calls=%async_computation.7 | async-start | bytes 8388608
  2378.0 9.9 slice-start.2
  2378.0 11.1 slice-start.3
  2389.1 6.2 copy-start.9
  (1 other events, 0.7 us)
Sparse Core Ops, SparseCore 0:
  39.6 233.9 all-gather.14
  275.4 231.1 all-gather.12
  509.0 231.1 all-gather.10
  741.8 231.1 all-gather.8
  2190.0 12.4 all-reduce.4
  2206.3 150.9 all-reduce.6

commit v2 on v1

--- a/solution.py
+++ b/solution.py
@@ -16,7 +16,7 @@
 GROWS = TOK * SUB
 ROWS = GRP * GROWS
 HALF = DM // 2
-PIECE, HALO = 256, 32
+PIECE, HALO, WROWS, DEPTH = 256, 32, 1024, 4
 KSTEP, STRIP = 1024, 32
 POS_ROWS = GROWS + 64
 COLS = DM // LANES
@@ -36,9 +36,6 @@
     return jax.ShapeDtypeStruct(shape, dtype)
 
 
-TOKEN = sds((SUB, LANES), F32)
-
-
 def cost(us):
     return pl.CostEstimate(flops=int(us * 1e9), bytes_accessed=int(us * 1e6), transcendentals=0)
 
@@ -52,20 +49,30 @@
 
 
 NTOK = TOK // TILE
-SEQ_BLOCK = pl.BlockSpec((SUB, TILE, DM), lambda g, t: (g, t, 0))
-ROW_BLOCK = pl.BlockSpec((SUB * TILE, DM), lambda g, t: (g * NTOK + t, 0))
-ONE_ROW = pl.BlockSpec((1, DM), lambda g, t: (0, 0))
-SUM_BLOCK = pl.BlockSpec((SUB, DM), lambda g, t: (0, 0))
+FULL_DN, FULL_Z = 20 * SUB * TILE, 24 * SUB * TILE
+NBLK = GRP * NTOK
+ONE_ROW = pl.BlockSpec((1, DM), lambda i: (0, 0))
+SUM_BLOCK = pl.BlockSpec((SUB, DM), lambda i: (0, 0))
 TURN = pltpu.VMEM((COLS, SUB * TILE, LANES), F32)
 
 
-def row_call(kernel, us, inputs, in_specs, out_specs, out_shape, turns):
-    return pl.pallas_call(kernel, grid=(GRP, NTOK), in_specs=in_specs, out_specs=out_specs, out_shape=out_shape, scratch_shapes=[TURN] * turns,
-                          compiler_params=params(), cost_estimate=cost(us))(*inputs)
+def seq_block(first):
+    return pl.BlockSpec((SUB, TILE, DM), lambda i: ((first + i) // NTOK, (first + i) % NTOK, 0))
+
+
+def row_call(kernel, us, blocks, inputs, in_specs, out_specs, out_shape, turns, whole=None):
+    first, last = blocks
+    alias = {}
+    if whole is not None:
+        alias = {len(inputs): 0}
+        inputs = (*inputs, whole)
+        in_specs = in_specs + [ANY]
+    return pl.pallas_call(kernel, grid=(last - first,), in_specs=in_specs, out_specs=out_specs, out_shape=out_shape, scratch_shapes=[TURN] * turns,
+                          input_output_aliases=alias, compiler_params=params(), cost_estimate=cost(us))(*inputs)
 
 
 def first_step():
-    return (pl.program_id(0) == 0) & (pl.program_id(1) == 0)
+    return pl.program_id(0) == 0
 
 
 def both(val):
@@ -105,12 +112,17 @@
         g_ref[:, cols] = sg_ref[j].astype(BF)
 
 
+ROW_BLOCK = pl.BlockSpec((SUB * TILE, DM), lambda i: (i, 0))
+
+
 def norm_call(x, gz, scale):
-    return row_call(norm_kernel, 60, (x, gz, scale), [SEQ_BLOCK, SEQ_BLOCK, ONE_ROW], [ROW_BLOCK, ROW_BLOCK, SUM_BLOCK],
+    seq = seq_block(0)
+    return row_call(norm_kernel, 60, (0, NBLK), (x, gz, scale), [seq, seq, ONE_ROW], [ROW_BLOCK, ROW_BLOCK, SUM_BLOCK],
                     [sds((ROWS, DM), BF), sds((ROWS, DM), BF), sds((SUB, DM), F32)], 2)
 
 
-def z_kernel(acc_ref, x_ref, bo_ref, z_ref, sa_ref):
+def z_kernel(acc_ref, x_ref, bo_ref, *refs):
+    z_ref, sa_ref = refs[-2:]
     for j, cols in lane_tiles():
         sa_ref[j] = acc_ref[:, cols]
     for b in range(SUB):
@@ -118,11 +130,14 @@
             z_ref[b, :, cols] = (x_ref[b, :, cols].astype(F32) + (sa_ref[j, pl.ds(b, TILE, stride=SUB), :] + bo_ref[:, cols])).astype(BF)
 
 
-def z_call(acc, x, b_out):
-    return row_call(z_kernel, 50, (acc, x, b_out), [ROW_BLOCK, SEQ_BLOCK, ONE_ROW], SEQ_BLOCK, sds((GRP * SUB, TOK, DM), BF), 1)
-
-
-def gx_kernel(dn_ref, x_ref, gz_ref, sc_ref, gx_ref, gs_ref, sa_ref):
+def z_call(blocks, acc, x, b_out, whole=None):
+    seq = seq_block(blocks[0])
+    return row_call(z_kernel, 40, blocks, (acc, x, b_out), [ROW_BLOCK, seq, ONE_ROW], seq, sds((GRP * SUB, TOK, DM), BF), 1, whole)
+
+
+def gx_kernel(dn_ref, x_ref, gz_ref, sc_ref, *refs):
+    gx_ref, gs_ref, sa_ref = refs[-3:]
+
     @pl.when(first_step())
     def _():
         gs_ref[...] = jnp.zeros_like(gs_ref)
@@ -146,44 +161,10 @@
         gs_ref[:, cols] = total
 
 
-def gx_call(dn, x, gz, scale):
-    return row_call(gx_kernel, 70, (dn, x, gz, scale), [ROW_BLOCK, SEQ_BLOCK, SEQ_BLOCK, ONE_ROW], [SEQ_BLOCK, SUM_BLOCK],
-                    [sds((GRP * SUB, TOK, DM), BF), sds((SUB, DM), F32)], 1)
-
-
-def cast_kernel(*refs):
-    outs, tok = refs[-4:-1], refs[-1]
-    tok[...] = jnp.zeros_like(tok)
-    for which in range(2):
-        @pl.when(pl.program_id(0) == which)
-        def _(which=which):
-            for kind in range(3):
-                outs[kind][...] = refs[3 * which + kind][0].astype(BF)
-
-
-def cast_call(phase, a_half, b_half, prev, after):
-    def half_row(s):
-        core = lax.axis_index("cp")
-        return core + s * (1 - 2 * core)
-
-    def half_spec(which, kind):
-        return pl.BlockSpec((1, HALF, CH), lambda s, r: ((r * s if which else r * (1 - s) + 3 * s), kind, 0))
-
-    in_specs = [half_spec(which, kind) for which in range(2) for kind in range(3)]
-    args = [a_half] * 3 + [b_half] * 3
-    alias = {}
-    if prev is not None:
-        alias = {len(args) + k: k for k in range(3)}
-        args += list(prev)
-        in_specs += [ANY] * 3
-    args += list(after)
-    in_specs += [ANY] * len(after)
-    *weights, tok = pl.pallas_call(
-        cast_kernel, grid=(2, 4), in_specs=in_specs,
-        out_specs=[pl.BlockSpec((HALF, CH), lambda s, r: (half_row(s), r * 2 + phase % 2))] * 3 + [pl.BlockSpec((SUB, LANES), lambda s, r: (0, 0))],
-        out_shape=[sds((DM, HALF), BF)] * 3 + [TOKEN], input_output_aliases=alias,
-        compiler_params=params(), cost_estimate=cost(25))(*args)
-    return weights, tok
+def gx_call(blocks, dn, x, gz, scale, whole=None):
+    seq = seq_block(blocks[0])
+    return row_call(gx_kernel, 50, blocks, (dn, x, gz, scale), [ROW_BLOCK, seq, seq, ONE_ROW], [seq, SUM_BLOCK],
+                    [sds((GRP * SUB, TOK, DM), BF), sds((SUB, DM), F32)], 1, whole)
 
 
 def run(steps):
@@ -201,20 +182,26 @@
     def take(count):
         return [next(it) for _ in range(count)]
 
-    n_hbm, g_hbm, wy_hbm, wx_hbm, wo_hbm = take(5)
-    gate_hbm = take(1 if own else 2)
+    n_hbm, g_hbm = take(2)
+    if own:
+        own_w = take(3)
+        gate_hbm = take(1)
+    else:
+        gate_hbm = take(2)
     par_ref, pos_ref = take(2)
+    if not own:
+        take(4)
+    mixed_hbm, dyx_hbm, wyx_hbm, wz_hbm = take(4)
+    outs = [mixed_hbm, dyx_hbm, dyx_hbm]
     if own:
-        outs = take(9)
+        outs += take(3)
         conv_hbm, dpre_hbm, stat_ref = take(3)
-    else:
-        take(3)
-        outs = take(3)
-    tok_ref, = take(1)
     nbuf, gbuf, wbuf, wgf, wgb, py, dm, xbuf, ab, uv, yb, w1b, pb, qab, qib, mib, dbuf, conv, pre, dpre, dconv, st_m, st_y, st_x, st1, st2, enter, csend, crecv = take(29)
     if own:
         rb = next(it)
-    n_sem, g_sem, w_sem, wg_sem, o_sem, c_send, c_recv, d_send, d_recv, x_send, x_recv = take(11)
+    if not own:
+        stage = next(it)
+    n_sem, g_sem, w_sem, wo_sem, wg_sem, o_sem, c_send, c_recv, d_send, d_recv, x_send, x_recv = take(12)
     if own:
         p_sem = next(it)
 
@@ -241,10 +228,98 @@
         src, dst, sem = ((n_hbm, nbuf, n_sem), (g_hbm, gbuf, g_sem))[which]
         return pltpu.make_async_copy(src.at[rows], dst.at[slot], sem.at[slot])
 
-    def weight_copy(blk, which):
+    blocks, turns = units // groups, groups * pieces
+
+    def weight_in(blk, kind):
         slot = lax.rem(blk, 2)
-        src = (wy_hbm, wx_hbm, wo_hbm)[which]
-        return pltpu.make_async_copy(src.at[:, pl.ds(al(col_of(blk, False) * CH, CH), CH)], wbuf.at[slot, which], w_sem.at[slot, which])
+        return pltpu.make_async_copy(own_w[kind].at[:, pl.ds(al(blk * CH, CH), CH)], wbuf.at[slot, kind], w_sem.at[slot, kind])
+
+    def weight_out(blk, kind):
+        slot = lax.rem(blk, 2)
+        col = col_of(blk, True) * CH + (DM if kind == 1 else 0)
+        dst = wz_hbm if kind == 2 else wyx_hbm
+        return pltpu.make_async_copy(wbuf.at[slot, kind], dst.at[:, pl.ds(al(col, CH), CH)], wo_sem.at[slot, kind])
+
+    per_half = 3 * HALF // WROWS
+
+    def strip_slot(t, half):
+        return lax.rem(t + half * per_half, DEPTH)
+
+    def strip_in(blk, t, half):
+        rows = pl.ds(al(t * WROWS, WROWS), WROWS)
+        return pltpu.make_async_copy(gate_hbm[half].at[chip_of(blk)[0], rows], stage.at[strip_slot(t, half)], w_sem.at[strip_slot(t, half)])
+
+    def strip_cast(blk, t, half):
+        per_kind = HALF // WROWS
+        row = (peer if half else core) * HALF + lax.rem(t, per_kind) * WROWS
+        wbuf[lax.rem(blk, 2), lax.div(t, per_kind), pl.ds(al(row, WROWS), WROWS), :] = stage[strip_slot(t, half)].astype(BF)
+
+    def weight_turn(q):
+        blk, t = lax.div(q, turns), lax.rem(q, turns)
+
+        @pl.when((t == 0) & (blk >= 1) & (blk + 1 < blocks))
+        def _():
+            for kind in range(3):
+                weight_out(blk - 1, kind).wait()
+
+        if own:
+            @pl.when(t == 0)
+            def _():
+                for kind in range(3):
+                    weight_in(blk, kind).wait()
+                    weight_out(blk, kind).start()
+
+                @pl.when(blk + 1 < blocks)
+                def _():
+                    for kind in range(3):
+                        weight_in(blk + 1, kind).start()
+
+            return
+        more = blk + 1 < blocks
+        for half in range(2):
+            done = t - 1 - half * per_half
+
+            @pl.when(more & (done >= 0) & (done < per_half))
+            def _(half=half, done=done):
+                strip_in(blk + 1, done, half).wait()
+                strip_cast(blk + 1, done, half)
+        for half in range(2):
+            new = t - half * per_half
+
+            @pl.when(more & (new >= 0) & (new < per_half))
+            def _(half=half, new=new):
+                strip_in(blk + 1, new, half).start()
+
+        @pl.when(more & (t == 2 * per_half + 1))
+        def _():
+            for kind in range(3):
+                weight_out(blk + 1, kind).start()
+
+    def weights_first():
+        if own:
+            for kind in range(3):
+                weight_in(0, kind).start()
+            return
+        ahead = DEPTH - 1
+        for t in range(ahead):
+            strip_in(0, t, 0).start()
+        for half in range(2):
+            def turn(t, _, half=half):
+                @pl.when(t + ahead < per_half)
+                def _():
+                    strip_in(0, t + ahead, half).start()
+
+                if half == 0:
+                    @pl.when(t + ahead >= per_half)
+                    def _():
+                        strip_in(0, t + ahead - per_half, 1).start()
+                strip_in(0, t, half).wait()
+                strip_cast(0, t, half)
+                return 0
+
+            lax.fori_loop(0, per_half, turn, 0)
+        for kind in range(3):
+            weight_out(0, kind).start()
 
     def gate_copies(blk):
         slot = lax.rem(blk, 2)
@@ -261,7 +336,7 @@
         slot = lax.rem(q, 2)
         src = (st_m, st_y, st_x)[which % 3].at[slot]
         rows = pl.ds(al(grp * GROWS + p * PIECE, PIECE), PIECE)
-        col = blk if which >= 6 else col_of(blk, True)
+        col = blk if which >= 3 else col_of(blk, True) + (DM // CH if which == 2 else 0)
         return pltpu.make_async_copy(src, outs[which].at[rows, pl.ds(al(col * CH, CH), CH)], o_sem.at[which, slot])
 
     def conv_copy(q):
@@ -270,7 +345,7 @@
         p = i + core * (pieces - 1 - 2 * i)
         slot = lax.rem(q, 2)
         rows = pl.ds(al(grp * GROWS + p * PIECE, PIECE), PIECE)
-        return pltpu.make_async_copy(conv.at[slot], conv_hbm.at[rows, pl.ds(al(blk * CH, CH), CH)], p_sem.at[0, slot])
+        return pltpu.make_async_copy(conv.at[slot], conv_hbm.at[blk, rows], p_sem.at[0, slot])
 
     def dpre_copy(q):
         u, i = unit_of(q - LAG_GRADS)
@@ -278,7 +353,7 @@
         p = i + peer * (pieces - 1 - 2 * i)
         slot = lax.rem(q, 2)
         rows = pl.ds(al(grp * GROWS + p * PIECE, PIECE), PIECE)
-        return pltpu.make_async_copy(dpre.at[slot], dpre_hbm.at[rows, pl.ds(al(blk * 2 * CH, CH), 2 * CH)], p_sem.at[1, slot])
+        return pltpu.make_async_copy(dpre.at[slot], dpre_hbm.at[blk, rows], p_sem.at[1, slot])
 
     def remote(src, dst, send, recv):
         return pltpu.make_async_remote_copy(src_ref=src, dst_ref=dst, send_sem=send, recv_sem=recv, device_id={"cp": peer}, device_id_type=pl.DeviceIdType.MESH)
@@ -301,9 +376,6 @@
         made = []
         for which in range(len(outs)):
             lag, forward, when = (LAG_DX, None, last) if which % 3 == 2 else (LAG_GRADS, peer, grads)
-            if own and which < 6:
-                late = q - lag >= steps // 2
-                when = when & (late if which >= 3 else ~late)
             made.append((when, functools.partial(out_copy, q, lag, which, forward)))
         if own:
             made += [((q >= LAG_TAPS) & (q < steps + LAG_TAPS), lambda: conv_copy(q)), (grads, lambda: dpre_copy(q))]
@@ -525,7 +597,7 @@
             wgb[slot, :, :CH] = wgf[slot, 0].astype(BF)
             wgb[slot, :, CH:] = wgf[slot, 1].astype(BF)
 
-            @pl.when(blk + 1 < units // groups)
+            @pl.when(blk + 1 < blocks)
             def _():
                 for cp in gate_copies(blk + 1):
                     cp.start()
@@ -550,11 +622,9 @@
 
     for which in range(2):
         row_copy(0, which).start()
-    for which in range(3):
-        weight_copy(0, which).start()
     for cp in gate_copies(0):
         cp.start()
-    tok_ref[...] = jnp.zeros_like(tok_ref)
+    weights_first()
     for slot in range(2):
         ab[slot, pl.ds(GROWS, SUB), :] = jnp.ones((SUB, CH), F32)
     if own:
@@ -572,17 +642,7 @@
             for which in range(2):
                 row_copy(q + 1, which).start()
 
-        @pl.when(lax.rem(q, groups * pieces) == 0)
-        def _():
-            blk = lax.div(q, groups * pieces)
-            for which in range(3):
-                weight_copy(blk, which).wait()
-
-            @pl.when(blk + 1 < units // groups)
-            def _():
-                for which in range(3):
-                    weight_copy(blk + 1, which).start()
-
+        weight_turn(q)
         start_of_step(q)
         product_steps, spent, made = products(q), share, 0
         for stage in (taps_back, back, grads, gates, taps):
@@ -608,6 +668,9 @@
         return 0
 
     lax.fori_loop(steps, steps + LAG_DX, drain_step, 0)
+    for blk in (blocks - 2, blocks - 1):
+        for kind in range(3):
+            weight_out(jnp.int32(blk), kind).wait()
     for q in (steps + LAG_DX, steps + LAG_DX + 1):
         for when, make in out_copies(jnp.int32(q - 2)):
             @pl.when(when)
@@ -615,7 +678,7 @@
                 make().wait()
 
 
-def rnn_call(phase, groups, n, gz, weights, gate_src, par, pos, acts):
+def rnn_call(phase, groups, n, gz, sources, par, pos, whole):
     own = phase is None
     units = (4 if own else 3) * groups
 
@@ -623,20 +686,16 @@
         return (0, blk) if own else (lax.rem(lax.axis_index("tp") + 1 + blk, 4), 0)
 
     def col_of(blk, merged):
-        if own:
-            return lax.axis_index("tp") * 2 + lax.rem(blk, 2) if merged else blk
-        return chip_of(blk)[0] * 2 + phase % 2
-
-    args = [n, gz, *weights, *gate_src, par, pos, *acts]
-    in_specs = [ANY] * (5 + len(gate_src)) + [VM] * 2 + [ANY] * len(acts)
-    out_specs = [ANY] * 3
-    out_shape = [sds((ROWS, HALF), BF)] * 3
-    alias = {9 + k: k for k in range(len(acts))}
+        return lax.axis_index("tp") * 4 + blk if own else chip_of(blk)[0] * 4 + phase
+
+    args = [n, gz, *sources, par, pos, *whole]
+    in_specs = [ANY] * (2 + len(sources)) + [VM] * 2 + [ANY] * len(whole)
+    out_specs = [ANY] * 4
+    out_shape = [sds((ROWS, DM), BF), sds((ROWS, 2 * DM), BF), sds((DM, 2 * DM), BF), sds((DM, DM), BF)]
+    alias = {6 + k: k for k in range(len(whole))}
     if own:
-        out_specs = [ANY] * 11 + [VM]
-        out_shape = out_shape * 2 + [sds((ROWS, 4 * CH), BF)] * 4 + [sds((ROWS, SUB * CH), BF), sds((4, 80, CH), F32)]
-    out_specs = out_specs + [VM]
-    out_shape = out_shape + [TOKEN]
+        out_specs = [ANY] * 9 + [VM]
+        out_shape = out_shape + [sds((ROWS, 4 * CH), BF)] * 3 + [sds((4, ROWS, CH), BF), sds((4, ROWS, 2 * CH), BF), sds((4, 10 * SUB, CH), F32)]
 
     def buf(slots, rows, dtype=F32, cols=CH):
         return pltpu.VMEM((slots, rows, cols), dtype)
@@ -647,10 +706,12 @@
                pltpu.VMEM((2, 2, GROWS + SUB, CH), F32)] + [buf(2, GROWS)] * 6 + [buf(2, GROWS + HALO), buf(2, PIECE, BF),
                pltpu.VMEM((PIECE + STRIP, 2 * CH), F32), buf(2, PIECE, BF, 2 * CH), piece32] + [buf(2, PIECE, BF)] * 3 + [pltpu.VMEM((SUB, CH), F32)] * 3 + [buf(2, SUB)] * 2
     dma = pltpu.SemaphoreType.DMA
-    sems = [dma((2,)), dma((2,)), dma((2, 3)), dma((2, 2)), dma((9 if own else 3, 2))] + [dma((2,))] * 6
+    sems = [dma((2,)), dma((2,)), dma((2, 3) if own else (DEPTH,)), dma((2, 3)), dma((2, 2)), dma((6 if own else 3, 2))] + [dma((2,))] * 6
     if own:
         scratch.append(buf(2, GROWS))
         sems.append(dma((2, 2)))
+    else:
+        scratch.append(buf(DEPTH, WROWS))
     return pl.pallas_call(
         functools.partial(rnn_kernel, own, groups, units, chip_of, col_of), in_specs=in_specs, out_specs=out_specs, out_shape=out_shape,
         scratch_shapes=scratch + sems, input_output_aliases=alias,
@@ -689,42 +750,42 @@
     scale = norm_scale.astype(F32)[None]
     n, gz, gb = norm_call(x_in, grad_z, scale)
 
-    first = rnn_call(None, GRP, n, gz, (w_y, w_x, w_out.T), (wg_own,), par_own[None], pos, ())
-    sets, (omixed, ody, odx, conv16, dpre16, stats) = [first[:3], first[3:6]], first[6:12]
-    weights = [None, None]
+    first = rnn_call(None, GRP, n, gz, (w_y, w_x, w_out.T, wg_own), par_own[None], pos, ())
+    whole, (omixed, ody, odx, conv16, dpre16, stats) = first[:4], first[4:]
 
     def dot(lhs, rhs, dims):
         return lax.dot_general(lhs, rhs, dims, preferred_element_type=F32)
 
-    def phase(j, deps):
-        s = j // 2
+    for j in range(4):
         other = partner(got[j])
-        weights[s], _ = cast_call(j, got[j], other, weights[s], deps)
-        par = got[j][:, None, 3 * HALF + CH:]
-        *acts, token = rnn_call(j, GRP, n, gz, weights[s], (got[j], other), par, pos, sets[s])
-        sets[s] = acts
-        return token
+        whole = rnn_call(j, GRP, n, gz, (got[j], other), got[j][:, None, 3 * HALF + CH:], pos, whole)
+    mixed, dyx, wyx, wz = whole
 
     g_w_x = dot(n, odx, TN)
     g_w_y = dot(n, ody, TN)
-    phase(0, (g_w_x, g_w_y))
     g_w_out = dot(omixed, gz, TN)
-    g_gate = 0.5 * jnp.einsum("rhk,rhj->hkj", conv16.reshape(ROWS, 4, CH), dpre16.reshape(ROWS, 4, 2 * CH), preferred_element_type=F32)
+    g_gate = 0.5 * jnp.einsum("hrk,hrj->hkj", conv16, dpre16, preferred_element_type=F32)
     stats = jnp.sum(stats.reshape(4, 10, SUB, CH), axis=2).transpose(1, 0, 2).reshape(10, 4 * CH)
-    phase(1, (g_w_out, g_gate))
     g_w_x, g_w_y, g_w_out, g_gate = lax.psum((g_w_x, g_w_y, g_w_out, g_gate), "cp")
-    z_acc = dot(sets[0][0], weights[0][2], NT)
-    dn = dot(sets[0][1], weights[0][0], NT)
-    dn = dot(sets[0][2], weights[0][1], NT) + dn
-    phase(2, (z_acc, dn))
-    phase(3, ())
-    z_acc = dot(sets[1][0], weights[1][2], NT) + z_acc
-    z_out = z_call(z_acc, x_in, b_out.astype(F32)[None])
-    dn = dot(sets[1][1], weights[1][0], NT) + dn
-    dn = dot(sets[1][2], weights[1][1], NT) + dn
-    grad_x, gs = gx_call(dn, x_in, grad_z, scale)
-
-    g_scale, stats, g_b_out = lax.psum((jnp.sum(gs, axis=0), stats, jnp.sum(gb, axis=0)), "cp")
+
+    def shared(acts, weight, full):
+        own_rows = (ROWS - full) // 4
+        mine = lax.dynamic_slice(acts, (full + lax.axis_index("tp") * own_rows, 0), (own_rows, acts.shape[1]))
+        mine = lax.optimization_barrier(dot(mine, weight, NT))
+        return lax.all_gather(mine, "tp", tiled=True)
+
+    bias = b_out.astype(F32)[None]
+    dn_mid, z_mid = FULL_DN // (SUB * TILE), FULL_Z // (SUB * TILE)
+    dn_rest, z_rest = shared(dyx, wyx, FULL_DN), shared(mixed, wz, FULL_Z)
+    grad_x, gs = gx_call((0, dn_mid), dot(dyx[:FULL_DN], wyx, NT), x_in, grad_z, scale)
+    grad_x, gs_rest = gx_call((dn_mid, NBLK), dn_rest, x_in, grad_z, scale, grad_x)
+    gs = gs + gs_rest
+    z_out = z_call((0, z_mid), dot(mixed[:FULL_Z], wz, NT), x_in, bias)
+    z_out = z_call((z_mid, NBLK), z_rest, x_in, bias, z_out)
+
+    sums = jnp.concatenate([jnp.sum(gs, axis=0), stats.reshape(-1), jnp.sum(gb, axis=0)])
+    sums = sums + partner(sums)
+    g_scale, stats, g_b_out = sums[:DM], sums[DM:-DM].reshape(10, 4 * CH), sums[-DM:]
     return (z_out, grad_x, g_scale, g_w_x, stats[4], g_w_y, stats[0], stats[6:10], stats[5], g_gate[:, :, :CH], 0.5 * stats[1],
             g_gate[:, :, CH:], 0.5 * stats[2], 4.0 * jax.nn.sigmoid(a_param) * stats[3], g_w_out, g_b_out)
 

time: 2410 us -> 2190 us (0.909)
  matrix products: 649 us -> 506 us
  Pallas kernels: 1150 us -> 1080 us
    dot_general x9 -> x7, matrix products: 635 us -> 492 us  [dot(): return lax.dot_general(lhs, rhs, dims, preferred_element_type=F32)]
    pallas_call x7 -> x5, Pallas kernels: 310 us -> 199 us  [row_call(): pl.pallas_call(kernel, grid=(last - first,), in_specs=in_specs, out_specs...]
    pallas_call x5, Pallas kernels: 839 us -> 879 us  [rnn_call(): pl.pallas_call(functools.partial(rnn_kernel, own, groups, units, chip_of,...]
    unnamed x53 -> x44, local copies, waits for them, and re-layouts: 49.4 us -> 47.9 us
  transfers between devices with their start and end apart: 11 -> 13, of which waited for: 4 -> 3; matrix products, arithmetic and copies ran while one was open for 21% -> 22% of each run, Pallas kernels for 37% -> 42%
where the time goes in v2:
time: 2190 us; the launch traced here: 2180 us
  Pallas kernels  1080 us (49%)
  matrix products  506 us (23%)
  waiting for transfers between devices  491 us (22%)
  local copies, waits for them, and re-layouts  61.9 us (3%)
  other arithmetic  28.6 us (1%)
    pallas_call x5, Pallas kernels, rnn_call(): pl.pallas_call(functools.partial(rnn_kernel, own, groups, units, chip_of,...  879 us
    dot_general x7, matrix products, dot(): return lax.dot_general(lhs, rhs, dims, preferred_element_type=F32)  492 us
    all_gather x4, waiting for transfers between devices, layer(): got.append(lax.all_gather(mine, 'tp'))  490 us
    pallas_call x5, Pallas kernels, row_call(): pl.pallas_call(kernel, grid=(last - first,), in_specs=in_specs, out_specs...  199 us
    unnamed x44, local copies, waits for them, and re-layouts  47.9 us
  transfers between devices with their start and end apart: 13, of which 3 were waited for; matrix products, arithmetic and copies ran while one was open for 22% of the time, Pallas kernels for 42%

profile of v2, /device:TPU:0, one launch (start us, length us, event | category | flops | bytes accessed | tf_op | source)
XLA Modules:
  0.0 2183.6 jit_solution(13155588179846262035)
XLA Ops:
  13.1 12.0 copy.96
  25.3 6.4 convert_dynamic-update-slice_fusion.1
  31.7 5.6 convert_dynamic-update-slice_fusion
  37.4 5.7 bitcast_dynamic-update-slice_fusion
  48.5 65.8 %shard_map.288 = (bf16[4096,4096]{1,0:T(8,128)(2,1)}, bf16[4096,4096]{1,0:T(8,128)(2,1)}, f32[8,4096]{1,0:T(8,128)}) custom-call(bf16[32,128,4096]{2,1,0:T(8,128)(2,1)} %x_ref.9, bf16[32,128,4096]{2,1,0:T(8,128)(2,1)} %gz_ref.5, f32[1,4096]{1,0:T(1,128)} %bitcast.117), custom_call_target="tpu_custom_call" | custom-call | flops 60000002048 | bytes 60000000 | tf_op jit(solution)/shard_map/pallas_call | solution.py:70
  114.6 2.0 broadcast_in_dim.41.refs_7_.refs_5_
  116.6 225.7 %shard_map.289 = (bf16[4096,4096]{1,0:T(8,128)(2,1)}, bf16[4096,8192]{1,0:T(8,128)(2,1)}, bf16[4096,8192]{1,0:T(8,128)(2,1)}, bf16[4096,4096]{1,0:T(8,128)(2,1)}...) custom-call(bf16[4096,4096]{1,0:T(8,128)(2,1)} %get-tuple-element.49, ...), custom_call_target="tpu_custom_call" | custom-call | flops 160000000000 | bytes 160000000 | tf_op jit(solution)/shard_map/pallas_call | solution.py:715
  342.4 14.1 convolution_multiply_fusion
  356.5 43.9 %fusion.22 = f32[1024,4096]{1,0:T(8,128)} fusion(bf16[4096,1024]{1,0:T(8,128)(2,1)} %get-tuple-element.81, bf16[4096,4096]{1,0:T(8,128)(2,1)} %get-tuple-element.50.refs_1_), kind=kOutput, calls=%fused_computation.64 | convolution fusion | flops 34359738368 | bytes 58720256 | tf_op jit(solution)/shard_map/dot_general | solution.py:757
  400.4 42.5 %fusion.20 = f32[4096,1024]{1,0:T(8,128)} fusion(bf16[4096,4096]{1,0:T(8,128)(2,1)} %get-tuple-element.49.refs_0_, bf16[4096,1024]{1,0:T(8,128)(2,1)S(1)} %copy-done.12), kind=kOutput, calls=%fused_computation.62 | convolution fusion | flops 34359738368 | bytes 58720256 | tf_op jit(solution)/shard_map/dot_general | solution.py:757
  442.9 42.5 %fusion.21 = f32[4096,1024]{1,0:T(8,128)} fusion(bf16[4096,4096]{1,0:T(8,128)(2,1)} %get-tuple-element.49.refs_0_, bf16[4096,1024]{1,0:T(8,128)(2,1)S(1)} %bitcast.140), kind=kOutput, calls=%fused_computation.63 | convolution fusion | flops 34359738368 | bytes 58720256 | tf_op jit(solution)/shard_map/dot_general | solution.py:757
  485.9 26.1 %all-gather.19.cloned.1.call-done = f32[25664,256]{1,0:T(8,128)} async-done(((f32[6416,256]{1,0:T(8,128)}), f32[25664,256]{1,0:T(8,128)}) %all-gather.19.cloned.1.call-update) | async-done | bytes 26279952 | tf_op jit(solution)/shard_map/all_gather | solution.py:740
  512.0 233.0 %all-gather.17.cloned.1.call-done = f32[25664,256]{1,0:T(8,128)} async-done(((f32[6416,256]{1,0:T(8,128)}), f32[25664,256]{1,0:T(8,128)}) %all-gather.17.cloned.1.call-update) | async-done | bytes 26279952 | tf_op jit(solution)/shard_map/all_gather | solution.py:740
  747.0 230.9 %all-gather.15.cloned.1.call-done = f32[25664,256]{1,0:T(8,128)} async-done(((f32[6416,256]{1,0:T(8,128)}), f32[25664,256]{1,0:T(8,128)}) %all-gather.15.cloned.1.call-update) | async-done | bytes 26279952 | tf_op jit(solution)/shard_map/all_gather | solution.py:740
  980.8 1.5 slice_bitcast_fusion.2.refs_4_
  983.7 3.0 fusion.17
  986.7 163.3 %shard_map.290 = (bf16[4096,4096]{1,0:T(8,128)(2,1)}, bf16[4096,8192]{1,0:T(8,128)(2,1)}, bf16[4096,8192]{1,0:T(8,128)(2,1)}, bf16[4096,4096]{1,0:T(8,128)(2,1)}) custom-call(bf16[4096,4096]{1,0:T(8,128)(2,1)} %get-tuple-element.49.refs_0_, ...), custom_call_target="tpu_custom_call", output_to_operand_aliasing={{0}: (6, {}), {1}: (7, {}), {2}: (8, {}), {3}: (9, {})} | custom-call | flops 120000004096 | bytes 120000000 | tf_op jit(solution)/shard_map/pallas_call | solution.py:715
  1150.0 163.1 %shard_map.291 = (bf16[4096,4096]{1,0:T(8,128)(2,1)}, bf16[4096,8192]{1,0:T(8,128)(2,1)}, bf16[4096,8192]{1,0:T(8,128)(2,1)}, bf16[4096,4096]{1,0:T(8,128)(2,1)}) custom-call(bf16[4096,4096]{1,0:T(8,128)(2,1)} %get-tuple-element.49.refs_0_, ...), custom_call_target="tpu_custom_call", output_to_operand_aliasing={{0}: (6, {}), {1}: (7, {}), {2}: (8, {}), {3}: (9, {})} | custom-call | flops 120000004096 | bytes 120000000 | tf_op jit(solution)/shard_map/pallas_call | solution.py:715
  1313.2 163.4 %shard_map.292 = (bf16[4096,4096]{1,0:T(8,128)(2,1)}, bf16[4096,8192]{1,0:T(8,128)(2,1)}, bf16[4096,8192]{1,0:T(8,128)(2,1)}, bf16[4096,4096]{1,0:T(8,128)(2,1)}) custom-call(bf16[4096,4096]{1,0:T(8,128)(2,1)} %get-tuple-element.49.refs_0_, ...), custom_call_target="tpu_custom_call", output_to_operand_aliasing={{0}: (6, {}), {1}: (7, {}), {2}: (8, {}), {3}: (9, {})} | custom-call | flops 120000004096 | bytes 120000000 | tf_op jit(solution)/shard_map/pallas_call | solution.py:715
  1476.5 163.1 %shard_map.293 = (bf16[4096,4096]{1,0:T(8,128)(2,1)}, bf16[4096,8192]{1,0:T(8,128)(2,1)}, bf16[4096,8192]{1,0:T(8,128)(2,1)}, bf16[4096,4096]{1,0:T(8,128)(2,1)}) custom-call(bf16[4096,4096]{1,0:T(8,128)(2,1)} %get-tuple-element.49.refs_0_, ...), custom_call_target="tpu_custom_call", output_to_operand_aliasing={{0}: (6, {}), {1}: (7, {}), {2}: (8, {}), {3}: (9, {})} | custom-call | flops 120000004096 | bytes 120000000 | tf_op jit(solution)/shard_map/pallas_call | solution.py:715
  1639.7 37.8 %fusion.4 = f32[384,4096]{1,0:T(8,128)} fusion(bf16[4096,8192]{1,0:T(8,128)(2,1)} %get-tuple-element.70, bf16[4096,8192]{1,0:T(8,128)(2,1)} %get-tuple-element.69, s32[]{:T(128)S(6)} %select_n.42), kind=kOutput, calls=%fused_computation.4 | convolution fusion | flops 25769803776 | bytes 79691776 | tf_op jit(solution)/shard_map/dot_general | solution.py:757
  1677.6 23.4 %fusion.6 = f32[256,4096]{1,0:T(8,128)} fusion(bf16[4096,4096]{1,0:T(8,128)(2,1)} %get-tuple-element.68, bf16[4096,4096]{1,0:T(8,128)(2,1)} %get-tuple-element.67, s32[]{:T(128)S(6)} %select_n.41), kind=kOutput, calls=%fused_computation.10 | convolution fusion | flops 8589934592 | bytes 39845892 | tf_op jit(solution)/shard_map/dot_general | solution.py:757
  1701.0 187.4 %fusion.dn_ref = f32[2560,4096]{1,0:T(8,128)} fusion(bf16[4096,8192]{1,0:T(8,128)(2,1)} %get-tuple-element.70, bf16[4096,8192]{1,0:T(8,128)(2,1)} %get-tuple-element.69), kind=kOutput, calls=%fused_computation | convolution fusion | flops 171798691840 | bytes 150994944 | tf_op jit(solution)/shard_map/dot_general | solution.py:757
  1888.4 114.1 %fusion.2.acc_ref = f32[3072,4096]{1,0:T(8,128)} fusion(bf16[4096,4096]{1,0:T(8,128)(2,1)} %get-tuple-element.68, bf16[4096,4096]{1,0:T(8,128)(2,1)} %get-tuple-element.67), kind=kOutput, calls=%fused_computation.2 | convolution fusion | flops 103079215104 | bytes 109051904 | tf_op jit(solution)/shard_map/dot_general | solution.py:757
  2002.4 42.1 %shard_map.294.refs_0_ = bf16[32,128,4096]{2,1,0:T(8,128)(2,1)} custom-call(f32[3072,4096]{1,0:T(8,128)} %fusion.2.acc_ref, bf16[32,128,4096]{2,1,0:T(8,128)(2,1)} %x_ref.9, f32[1,4096]{1,0:T(1,128)} %bitcast.120), custom_call_target="tpu_custom_call" | custom-call | flops 40000000000 | bytes 40000000 | tf_op jit(solution)/shard_map/pallas_call | solution.py:70
  2044.5 47.0 %shard_map.296 = (bf16[32,128,4096]{2,1,0:T(8,128)(2,1)}, f32[8,4096]{1,0:T(8,128)}) custom-call(f32[2560,4096]{1,0:T(8,128)} %fusion.dn_ref, bf16[32,128,4096]{2,1,0:T(8,128)(2,1)} %x_ref.9, bf16[32,128,4096]{2,1,0:T(8,128)(2,1)} %gz_ref.5, f32[1,4096]{1,0:T(1,128)} %bitcast.118), custom_call_target="tpu_custom_call" | custom-call | flops 49999998976 | bytes 50000000 | tf_op jit(solution)/shard_map/pallas_call | solution.py:70
  2091.5 29.2 %shard_map.297 = (bf16[32,128,4096]{2,1,0:T(8,128)(2,1)}, f32[8,4096]{1,0:T(8,128)}) custom-call(f32[1536,4096]{1,0:T(8,128)} %all-gather.13.cloned.1.call-done.dn_ref, bf16[32,128,4096]{2,1,0:T(8,128)(2,1)} %x_ref.9, bf16[32,128,4096]{2,1,0:T(8,128)(2,1)} %gz_ref.5, f32[1,4096]{1,0:T(1,128)} %bitcast.119, ...), custom_call_target="tpu_custom_call", output_to_operand_aliasing={{0}: (4, {})} | custom-call | flops 49999998976 | bytes 50000000 | tf_op jit(solution)/shard_map/pallas_call | solution.py:70
  2124.1 14.8 shard_map.295
  2142.3 13.7 copy.146
  2156.0 2.7 copy-done
  2158.8 8.5 copy.147
  2169.8 6.2 copy.148
  (101 shorter events, 27.1 us)
Async XLA Ops:
  8.0 477.5 %all-gather.21.cloned.1.call-start = ((), (), s32[]{:S(2)}) async-start(), calls=%async_computation.5 | async-start | bytes 32849920 | tf_op jit(solution)/shard_map/all_gather | solution.py:740
  13.1 12.0 copy-start.2
  13.1 12.0 copy-start.3
  25.3 17.8 copy-start.1
  44.2 2.2 copy-start.6
  44.8 1.6 copy-start.9
  44.8 467.2 %all-gather.19.cloned.1.call-start = ((), (), s32[]{:S(2)}) async-start(), calls=%async_computation.4 | async-start | bytes 32849920 | tf_op jit(solution)/shard_map/all_gather | solution.py:740
  44.9 3.0 copy-start.10
  45.6 699.4 %all-gather.17.cloned.1.call-start = ((), (), s32[]{:S(2)}) async-start(), calls=%async_computation.3 | async-start | bytes 32849920 | tf_op jit(solution)/shard_map/all_gather | solution.py:740
  46.3 931.5 %all-gather.15.cloned.1.call-start = ((), (), s32[]{:S(2)}) async-start(), calls=%async_computation.2 | async-start | bytes 32849920 | tf_op jit(solution)/shard_map/all_gather | solution.py:740
  46.4 67.9 %collective-permute-start.1 = (s32[32,8]{1,0:T(8,128)S(1)}, s32[32,8]{1,0:T(8,128)S(1)}, u32[]{:S(2)}, u32[]{:S(2)}) collective-permute-start(s32[32,8]{1,0:T(8,128)S(1)} %bitcast.122), channel_id=1, source_target_pairs={{0,1},{1,0},{2,3},{3,2},{4,5},{5,4},{6,7},{7,6}} | collective-permute-start | bytes 3080 | tf_op jit(solution)/shard_map/ppermute | solution.py:743
  47.3 936.5 %all-reduce.3.cloned.1.call-start = ((), (), s32[]{:S(2)}) async-start(), calls=%async_computation.6 | async-start | bytes 104857600 | tf_op jit(solution)/shard_map/psum | solution.py:769
  356.5 43.9 %copy-start.12 = (bf16[4096,1024]{1,0:T(8,128)(2,1)S(1)}, bf16[4096,1024]{1,0:T(8,128)(2,1)}, u32[]{:S(2)}) copy-start(bf16[4096,1024]{1,0:T(8,128)(2,1)} %get-tuple-element.77) | copy-start | bytes 25165828
  356.5 86.4 %slice-start.4 = ((s8[8388608]{0:T(1024)(128)(4,1)}), s8[4194304]{0:T(1024)(128)(4,1)S(1)}, s32[]{:S(2)}) async-start(s8[8388608]{0:T(1024)(128)(4,1)} %bitcast.139), calls=%async_computation.11 | async-start | bytes 8388608
  400.4 42.5 %slice-start.5 = ((s8[8388608]{0:T(1024)(128)(4,1)}), s8[4194304]{0:T(1024)(128)(4,1)S(1)}, s32[]{:S(2)}) async-start(s8[8388608]{0:T(1024)(128)(4,1)} %bitcast.139), calls=%async_computation.12 | async-start | bytes 8388608
  485.4 259.6 %copy-start.8 = (f32[8,4096]{1,0:T(8,128)S(1)}, f32[8,4096]{1,0:T(8,128)}, u32[]{:S(2)}) copy-start(f32[8,4096]{1,0:T(8,128)} %get-tuple-element.76) | copy-start | bytes 393220
  485.4 260.3 %copy-start.11 = (bf16[4096]{0:T(1024)(128)(2,1)S(1)}, bf16[4096]{0:T(1024)(128)(2,1)}, u32[]{:S(2)}) copy-start(bf16[4096]{0:T(1024)(128)(2,1)} %param.33) | copy-start | bytes 24580
  485.4 260.9 %copy-start.5 = (f32[4,80,256]{2,1,0:T(8,128)S(1)}, f32[4,80,256]{2,1,0:T(8,128)}, u32[]{:S(2)}) copy-start(f32[4,80,256]{2,1,0:T(8,128)} %get-tuple-element.75) | copy-start | bytes 983044
  485.4 1606.1 %all-gather.13.cloned.1.call-start = ((), (), s32[]{:S(2)}) async-start(), calls=%async_computation.1 | async-start | bytes 31457280 | tf_op jit(solution)/shard_map/all_gather | solution.py:775
  485.5 501.2 %collective-permute-start.4 = (f32[4,6416,256]{2,1,0:T(8,128)}, f32[4,6416,256]{2,1,0:T(8,128)}, u32[]{:S(2)}, u32[]{:S(2)}) collective-permute-start(f32[4,6416,256]{2,1,0:T(8,128)} %bitcast.136), channel_id=1, source_target_pairs={{0,1},{1,0},{2,3},{3,2},{4,5},{5,4},{6,7},{7,6}} | collective-permute-start | bytes 78839816 | tf_op jit(solution)/shard_map/ppermute | solution.py:743
  512.0 638.0 %collective-permute-start.3 = (f32[4,6416,256]{2,1,0:T(8,128)}, f32[4,6416,256]{2,1,0:T(8,128)}, u32[]{:S(2)}, u32[]{:S(2)}) collective-permute-start(f32[4,6416,256]{2,1,0:T(8,128)} %bitcast.133), channel_id=1, source_target_pairs={{0,1},{1,0},{2,3},{3,2},{4,5},{5,4},{6,7},{7,6}} | collective-permute-start | bytes 78839816 | tf_op jit(solution)/shard_map/ppermute | solution.py:743
  745.0 568.1 %collective-permute-start.2 = (f32[4,6416,256]{2,1,0:T(8,128)}, f32[4,6416,256]{2,1,0:T(8,128)}, u32[]{:S(2)}, u32[]{:S(2)}) collective-permute-start(f32[4,6416,256]{2,1,0:T(8,128)} %bitcast.130), channel_id=1, source_target_pairs={{0,1},{1,0},{2,3},{3,2},{4,5},{5,4},{6,7},{7,6}} | collective-permute-start | bytes 78839816 | tf_op jit(solution)/shard_map/ppermute | solution.py:743
  977.9 498.6 %collective-permute-start = (f32[4,6416,256]{2,1,0:T(8,128)}, f32[4,6416,256]{2,1,0:T(8,128)}, u32[]{:S(2)}, u32[]{:S(2)}) collective-permute-start(f32[4,6416,256]{2,1,0:T(8,128)} %bitcast.127), channel_id=1, source_target_pairs={{0,1},{1,0},{2,3},{3,2},{4,5},{5,4},{6,7},{7,6}} | collective-permute-start | bytes 78839816 | tf_op jit(solution)/shard_map/ppermute | solution.py:743
  1677.5 446.6 %all-gather.11.cloned.1.call-start = ((), (), s32[]{:S(2)}) async-start(), calls=%async_computation | async-start | bytes 20971520 | tf_op jit(solution)/shard_map/all_gather | solution.py:775
  2091.5 30.9 %copy-start.4 = (f32[10,2,4,128]{3,1,2,0:T(2,128)S(1)}, f32[10,2,4,128]{3,1,2,0:T(2,128)}, u32[]{:S(2)}) copy-start(f32[10,2,4,128]{3,1,2,0:T(2,128)} %copy.105) | copy-start | bytes 122884
  2121.8 0.6 copy-start.7
  2123.8 15.1 collective-permute-start.5
  2142.3 16.4 copy-start
  2142.3 24.9 %slice-start = ((s8[16777216]{0:T(1024)(128)(4,1)}), s8[4194304]{0:T(1024)(128)(4,1)S(1)}, s32[]{:S(2)}) async-start(s8[16777216]{0:T(1024)(128)(4,1)} %bitcast.100), calls=%async_computation.7 | async-start | bytes 8388608
  2142.3 24.9 %slice-start.1 = ((s8[16777216]{0:T(1024)(128)(4,1)}), s8[4194304]{0:T(1024)(128)(4,1)S(1)}, s32[]{:S(2)}) async-start(s8[16777216]{0:T(1024)(128)(4,1)} %bitcast.100), calls=%async_computation.8 | async-start | bytes 8388608
  2158.8 9.9 slice-start.2
  2158.8 11.1 slice-start.3
Sparse Core Ops, SparseCore 0:
  45.0 233.9 all-gather.20
  280.8 231.1 all-gather.18
  513.8 231.1 all-gather.16
  746.7 231.1 all-gather.14
  1677.6 222.1 all-gather.12
  1902.0 151.7 all-gather.10
Sparse Core Ops, SparseCore 1:
  485.5 161.8 all-reduce.2

commit v3 on v2

--- a/solution.py
+++ b/solution.py
@@ -48,7 +48,7 @@
     return [(j, slice(j * LANES, (j + 1) * LANES)) for j in range(COLS)]
 
 
-NTOK = TOK // TILE
+NTOK, WIDE = TOK // TILE, 512
 FULL_DN, FULL_Z = 20 * SUB * TILE, 24 * SUB * TILE
 NBLK = GRP * NTOK
 ONE_ROW = pl.BlockSpec((1, DM), lambda i: (0, 0))
@@ -133,6 +133,30 @@
 def z_call(blocks, acc, x, b_out, whole=None):
     seq = seq_block(blocks[0])
     return row_call(z_kernel, 40, blocks, (acc, x, b_out), [ROW_BLOCK, seq, ONE_ROW], seq, sds((GRP * SUB, TOK, DM), BF), 1, whole)
+
+
+def proj_kernel(act_ref, w_ref, x_ref, bo_ref, z_ref, sa_ref):
+    tok = x_ref.shape[1]
+    for half in range(0, WIDE, CH):
+        acc = lax.dot_general(act_ref[...], w_ref[half:half + CH], NT, preferred_element_type=F32)
+        for j in range(CH // LANES):
+            sa_ref[half // LANES + j] = acc[:, j * LANES:(j + 1) * LANES]
+    for b in range(SUB):
+        for j in range(WIDE // LANES):
+            cols = slice(j * LANES, (j + 1) * LANES)
+            out = x_ref[b, :, cols].astype(F32) + (sa_ref[j, pl.ds(b, tok, stride=SUB), :] + bo_ref[:, cols])
+            z_ref[b, :, cols] = out.astype(BF)
+
+
+def proj_call(rows, acts, weight, x, b_out):
+    tok = WIDE // SUB
+    per = TOK // tok
+    seq = pl.BlockSpec((SUB, tok, WIDE), lambda n, m: (m // per, m % per, n))
+    return pl.pallas_call(
+        proj_kernel, grid=(DM // WIDE, rows // WIDE),
+        in_specs=[pl.BlockSpec((WIDE, DM), lambda n, m: (m, 0)), pl.BlockSpec((WIDE, DM), lambda n, m: (n, 0)), seq, pl.BlockSpec((1, WIDE), lambda n, m: (0, n))],
+        out_specs=seq, out_shape=sds((GRP * SUB, TOK, DM), BF), scratch_shapes=[pltpu.VMEM((WIDE // LANES, WIDE, LANES), F32)],
+        compiler_params=params(), cost_estimate=cost(130), name="proj_z")(acts, weight, x, b_out)
 
 
 def gx_kernel(dn_ref, x_ref, gz_ref, sc_ref, *refs):
@@ -734,8 +758,11 @@
     got = []
     for j in range(4):
         cols = j * CH
+        rows_out = lax.dynamic_slice(w_out, (cols, half), (CH, HALF))
+        if j == 0:
+            rows_out = lax.optimization_barrier(rows_out)
         parts = [lax.dynamic_slice(w_y, (half, cols), (HALF, CH)).astype(F32), lax.dynamic_slice(w_x, (half, cols), (HALF, CH)).astype(F32),
-                 lax.dynamic_slice(w_out, (cols, half), (CH, HALF)).T.astype(F32), wg_mine[j], par_own[j]]
+                 rows_out.T.astype(F32), wg_mine[j], par_own[j]]
         mine = lax.optimization_barrier(jnp.concatenate(parts, axis=0))
         got.append(lax.all_gather(mine, "tp"))
 
@@ -766,7 +793,12 @@
     g_w_out = dot(omixed, gz, TN)
     g_gate = 0.5 * jnp.einsum("hrk,hrj->hkj", conv16, dpre16, preferred_element_type=F32)
     stats = jnp.sum(stats.reshape(4, 10, SUB, CH), axis=2).transpose(1, 0, 2).reshape(10, 4 * CH)
-    g_w_x, g_w_y, g_w_out, g_gate = lax.psum((g_w_x, g_w_y, g_w_out, g_gate), "cp")
+
+    def merged(val):
+        theirs = partner(val)
+        return val + theirs
+
+    g_w_x, g_w_y, g_w_out, g_gate = merged(g_w_x), merged(g_w_y), merged(g_w_out), merged(g_gate)
 
     def shared(acts, weight, full):
         own_rows = (ROWS - full) // 4
@@ -780,11 +812,11 @@
     grad_x, gs = gx_call((0, dn_mid), dot(dyx[:FULL_DN], wyx, NT), x_in, grad_z, scale)
     grad_x, gs_rest = gx_call((dn_mid, NBLK), dn_rest, x_in, grad_z, scale, grad_x)
     gs = gs + gs_rest
-    z_out = z_call((0, z_mid), dot(mixed[:FULL_Z], wz, NT), x_in, bias)
+    z_out = proj_call(FULL_Z, mixed, wz, x_in, bias)
     z_out = z_call((z_mid, NBLK), z_rest, x_in, bias, z_out)
 
     sums = jnp.concatenate([jnp.sum(gs, axis=0), stats.reshape(-1), jnp.sum(gb, axis=0)])
-    sums = sums + partner(sums)
+    sums = merged(sums)
     g_scale, stats, g_b_out = sums[:DM], sums[DM:-DM].reshape(10, 4 * CH), sums[-DM:]
     return (z_out, grad_x, g_scale, g_w_x, stats[4], g_w_y, stats[0], stats[6:10], stats[5], g_gate[:, :, :CH], 0.5 * stats[1],
             g_gate[:, :, CH:], 0.5 * stats[2], 4.0 * jax.nn.sigmoid(a_param) * stats[3], g_w_out, g_b_out)

time: 2190 us -> 2350 us (1.073)
  waiting for transfers between devices: 491 us -> 647 us
  matrix products: 506 us -> 389 us
  Pallas kernels: 1080 us -> 1180 us
  other arithmetic: 28.6 us -> 78.8 us
  local copies, waits for them, and re-layouts: 61.9 us -> 27.3 us
    all_gather x4, waiting for transfers between devices: 490 us -> 631 us  [layer(): got.append(lax.all_gather(mine, 'tp'))]
    pallas_call x0 -> x1, Pallas kernels: none -> 137 us  [proj_call(): pl.pallas_call(proj_kernel, grid=(DM // WIDE, rows // WIDE), in_specs=[pl...]
    dot_general x7 -> x6, matrix products: 492 us -> 377 us  [dot(): return lax.dot_general(lhs, rhs, dims, preferred_element_type=F32)]
    add x1 -> x5, other arithmetic: 0.9 us -> 55.3 us  [merged(): return val + theirs]
    pallas_call x5 -> x4, Pallas kernels: 199 us -> 157 us  [row_call(): pl.pallas_call(kernel, grid=(last - first,), in_specs=in_specs, out_specs...]
    unnamed x44 -> x43, local copies, waits for them, and re-layouts: 47.9 us -> 14.3 us
  transfers between devices with their start and end apart: 13 -> 16, of which waited for: 3 -> 4; matrix products, arithmetic and copies ran while one was open for 22% -> 18% of each run, Pallas kernels for 42% -> 44%
where the time goes in v3:
time: 2350 us; the launch traced here: 2340 us
  Pallas kernels  1180 us (50%)
  waiting for transfers between devices  647 us (28%)
  matrix products  389 us (17%)
  other arithmetic  78.8 us (3%)
  local copies, waits for them, and re-layouts  27.3 us (1%)
    pallas_call x5, Pallas kernels, rnn_call(): pl.pallas_call(functools.partial(rnn_kernel, own, groups, units, chip_of,...  888 us
    all_gather x4, waiting for transfers between devices, layer(): got.append(lax.all_gather(mine, 'tp'))  631 us
    dot_general x6, matrix products, dot(): return lax.dot_general(lhs, rhs, dims, preferred_element_type=F32)  377 us
    pallas_call x4, Pallas kernels, row_call(): pl.pallas_call(kernel, grid=(last - first,), in_specs=in_specs, out_specs...  157 us
    pallas_call x1, Pallas kernels, proj_call(): pl.pallas_call(proj_kernel, grid=(DM // WIDE, rows // WIDE), in_specs=[pl...  137 us
    add x5, other arithmetic, merged(): return val + theirs  55.3 us
  transfers between devices with their start and end apart: 16, of which 4 were waited for; matrix products, arithmetic and copies ran while one was open for 18% of the time, Pallas kernels for 44%

profile of v3, /device:TPU:0, one launch (start us, length us, event | category | flops | bytes accessed | tf_op | source)
XLA Modules:
  0.0 2341.9 jit_solution(16440367631456277991)
XLA Ops:
  7.2 11.9 copy.96
  19.2 5.8 convert_dynamic-update-slice_fusion.1
  26.8 6.5 convert_dynamic-update-slice_fusion
  33.3 5.4 bitcast_dynamic-update-slice_fusion.1
  43.1 231.5 %all-gather.21.cloned.1.call-done = f32[25664,256]{1,0:T(8,128)} async-done(((f32[6416,256]{1,0:T(8,128)}), f32[25664,256]{1,0:T(8,128)}) %all-gather.21.cloned.1.call-update) | async-done | bytes 26279952 | tf_op jit(solution)/shard_map/all_gather | solution.py:767
  275.7 65.4 %shard_map.288 = (bf16[4096,4096]{1,0:T(8,128)(2,1)}, bf16[4096,4096]{1,0:T(8,128)(2,1)}, f32[8,4096]{1,0:T(8,128)}) custom-call(bf16[32,128,4096]{2,1,0:T(8,128)(2,1)} %x_ref.9, bf16[32,128,4096]{2,1,0:T(8,128)(2,1)} %gz_ref.5, f32[1,4096]{1,0:T(1,128)} %bitcast.113), custom_call_target="tpu_custom_call" | custom-call | flops 60000002048 | bytes 60000000 | tf_op jit(solution)/shard_map/pallas_call | solution.py:70
  341.4 166.7 %all-gather.19.cloned.1.call-done = f32[25664,256]{1,0:T(8,128)} async-done(((f32[6416,256]{1,0:T(8,128)}), f32[25664,256]{1,0:T(8,128)}) %all-gather.19.cloned.1.call-update) | async-done | bytes 26279952 | tf_op jit(solution)/shard_map/all_gather | solution.py:767
  508.1 233.0 %all-gather.17.cloned.1.call-done = f32[25664,256]{1,0:T(8,128)} async-done(((f32[6416,256]{1,0:T(8,128)}), f32[25664,256]{1,0:T(8,128)}) %all-gather.17.cloned.1.call-update) | async-done | bytes 26279952 | tf_op jit(solution)/shard_map/all_gather | solution.py:767
  741.2 2.0 broadcast_in_dim.41.refs_7_.refs_5_
  743.2 232.9 %shard_map.289 = (bf16[4096,4096]{1,0:T(8,128)(2,1)}, bf16[4096,8192]{1,0:T(8,128)(2,1)}, bf16[4096,8192]{1,0:T(8,128)(2,1)}, bf16[4096,4096]{1,0:T(8,128)(2,1)}...) custom-call(bf16[4096,4096]{1,0:T(8,128)(2,1)} %get-tuple-element.49, ...), custom_call_target="tpu_custom_call" | custom-call | flops 160000000000 | bytes 160000000 | tf_op jit(solution)/shard_map/pallas_call | solution.py:739
  976.5 1.5 slice_bitcast_fusion.refs_4_
  982.4 165.9 %shard_map.290 = (bf16[4096,4096]{1,0:T(8,128)(2,1)}, bf16[4096,8192]{1,0:T(8,128)(2,1)}, bf16[4096,8192]{1,0:T(8,128)(2,1)}, bf16[4096,4096]{1,0:T(8,128)(2,1)}) custom-call(bf16[4096,4096]{1,0:T(8,128)(2,1)} %get-tuple-element.49.refs_0_, ...), custom_call_target="tpu_custom_call", output_to_operand_aliasing={{0}: (6, {}), {1}: (7, {}), {2}: (8, {}), {3}: (9, {})} | custom-call | flops 120000004096 | bytes 120000000 | tf_op jit(solution)/shard_map/pallas_call | solution.py:739
  1148.3 163.1 %shard_map.291 = (bf16[4096,4096]{1,0:T(8,128)(2,1)}, bf16[4096,8192]{1,0:T(8,128)(2,1)}, bf16[4096,8192]{1,0:T(8,128)(2,1)}, bf16[4096,4096]{1,0:T(8,128)(2,1)}) custom-call(bf16[4096,4096]{1,0:T(8,128)(2,1)} %get-tuple-element.49.refs_0_, ...), custom_call_target="tpu_custom_call", output_to_operand_aliasing={{0}: (6, {}), {1}: (7, {}), {2}: (8, {}), {3}: (9, {})} | custom-call | flops 120000004096 | bytes 120000000 | tf_op jit(solution)/shard_map/pallas_call | solution.py:739
  1311.4 163.1 %shard_map.292 = (bf16[4096,4096]{1,0:T(8,128)(2,1)}, bf16[4096,8192]{1,0:T(8,128)(2,1)}, bf16[4096,8192]{1,0:T(8,128)(2,1)}, bf16[4096,4096]{1,0:T(8,128)(2,1)}) custom-call(bf16[4096,4096]{1,0:T(8,128)(2,1)} %get-tuple-element.49.refs_0_, ...), custom_call_target="tpu_custom_call", output_to_operand_aliasing={{0}: (6, {}), {1}: (7, {}), {2}: (8, {}), {3}: (9, {})} | custom-call | flops 120000004096 | bytes 120000000 | tf_op jit(solution)/shard_map/pallas_call | solution.py:739
  1474.6 163.3 %shard_map.293 = (bf16[4096,4096]{1,0:T(8,128)(2,1)}, bf16[4096,8192]{1,0:T(8,128)(2,1)}, bf16[4096,8192]{1,0:T(8,128)(2,1)}, bf16[4096,4096]{1,0:T(8,128)(2,1)}) custom-call(bf16[4096,4096]{1,0:T(8,128)(2,1)} %get-tuple-element.49.refs_0_, ...), custom_call_target="tpu_custom_call", output_to_operand_aliasing={{0}: (6, {}), {1}: (7, {}), {2}: (8, {}), {3}: (9, {})} | custom-call | flops 120000004096 | bytes 120000000 | tf_op jit(solution)/shard_map/pallas_call | solution.py:739
  1637.9 37.7 %fusion.2 = f32[384,4096]{1,0:T(8,128)} fusion(bf16[4096,8192]{1,0:T(8,128)(2,1)} %get-tuple-element.70, bf16[4096,8192]{1,0:T(8,128)(2,1)} %get-tuple-element.69, s32[]{:T(128)S(6)} %select_n.42), kind=kOutput, calls=%fused_computation.2 | convolution fusion | flops 25769803776 | bytes 79691776 | tf_op jit(solution)/shard_map/dot_general | solution.py:784
  1675.8 45.9 %fusion.18 = f32[4096,1024]{1,0:T(8,128)} fusion(bf16[4096,4096]{1,0:T(8,128)(2,1)} %get-tuple-element.49.refs_0_, bf16[4096,1024]{1,0:T(8,128)(2,1)} %get-tuple-element.77), kind=kOutput, calls=%fused_computation.61 | convolution fusion | flops 34359738368 | bytes 58720256 | tf_op jit(solution)/shard_map/dot_general | solution.py:784
  1721.9 44.9 %fusion.19 = f32[4096,1024]{1,0:T(8,128)} fusion(bf16[4096,4096]{1,0:T(8,128)(2,1)} %get-tuple-element.49.refs_0_, bf16[4096,1024]{1,0:T(8,128)(2,1)} %get-tuple-element.78), kind=kOutput, calls=%fused_computation.62 | convolution fusion | flops 34359738368 | bytes 58720256 | tf_op jit(solution)/shard_map/dot_general | solution.py:784
  1767.2 43.1 %fusion.20 = f32[1024,4096]{1,0:T(8,128)} fusion(bf16[4096,1024]{1,0:T(8,128)(2,1)S(1)} %bitcast.136, bf16[4096,4096]{1,0:T(8,128)(2,1)} %get-tuple-element.50.refs_1_), kind=kOutput, calls=%fused_computation.63 | convolution fusion | flops 34359738368 | bytes 58720256 | tf_op jit(solution)/shard_map/dot_general | solution.py:784
  1810.5 11.7 convolution_multiply_fusion
  1824.5 14.2 collective-permute-done.8
  1838.7 2.1 add.62
  1840.8 1.5 fusion.15
  1842.3 17.3 add.60
  1859.6 17.1 add.61
  1876.7 17.9 add.64
  1894.6 17.5 fusion.4
  1912.1 187.7 %fusion.dn_ref = f32[2560,4096]{1,0:T(8,128)} fusion(bf16[4096,8192]{1,0:T(8,128)(2,1)} %get-tuple-element.70, bf16[4096,8192]{1,0:T(8,128)(2,1)} %get-tuple-element.69), kind=kOutput, calls=%fused_computation | convolution fusion | flops 171798691840 | bytes 150994944 | tf_op jit(solution)/shard_map/dot_general | solution.py:784
  2099.8 47.3 %shard_map.295 = (bf16[32,128,4096]{2,1,0:T(8,128)(2,1)}, f32[8,4096]{1,0:T(8,128)}) custom-call(f32[2560,4096]{1,0:T(8,128)} %fusion.dn_ref, bf16[32,128,4096]{2,1,0:T(8,128)(2,1)} %x_ref.9, bf16[32,128,4096]{2,1,0:T(8,128)(2,1)} %gz_ref.5, f32[1,4096]{1,0:T(1,128)} %bitcast.114), custom_call_target="tpu_custom_call" | custom-call | flops 49999998976 | bytes 50000000 | tf_op jit(solution)/shard_map/pallas_call | solution.py:70
  2147.0 137.2 %proj_z.1.refs_0_ = bf16[32,128,4096]{2,1,0:T(8,128)(2,1)} custom-call(bf16[4096,4096]{1,0:T(8,128)(2,1)} %get-tuple-element.67.act_ref, bf16[4096,4096]{1,0:T(8,128)(2,1)} %get-tuple-element.68.w_ref, bf16[32,128,4096]{2,1,0:T(8,128)(2,1)} %x_ref.9, f32[1,4096]{1,0:T(1,128)} %bitcast.116), custom_call_target="tpu_custom_call" | custom-call | flops 130000003072 | bytes 130000000 | tf_op jit(solution)/shard_map/proj_z/pallas_call | solution.py:155
  2284.2 29.2 %shard_map.296 = (bf16[32,128,4096]{2,1,0:T(8,128)(2,1)}, f32[8,4096]{1,0:T(8,128)}) custom-call(f32[1536,4096]{1,0:T(8,128)} %all-gather.13.cloned.1.call-done.dn_ref, bf16[32,128,4096]{2,1,0:T(8,128)(2,1)} %x_ref.9, bf16[32,128,4096]{2,1,0:T(8,128)(2,1)} %gz_ref.5, f32[1,4096]{1,0:T(1,128)} %bitcast.115, ...), custom_call_target="tpu_custom_call", output_to_operand_aliasing={{0}: (4, {})} | custom-call | flops 49999998976 | bytes 50000000 | tf_op jit(solution)/shard_map/pallas_call | solution.py:70
  2316.6 14.8 shard_map.294
  (108 shorter events, 21.9 us)
Async XLA Ops:
  7.2 267.4 %all-gather.21.cloned.1.call-start = ((), (), s32[]{:S(2)}) async-start(), calls=%async_computation.5 | async-start | bytes 32849920 | tf_op jit(solution)/shard_map/all_gather | solution.py:767
  19.2 7.2 copy-start.14
  19.2 7.3 copy-start.10
  19.2 7.3 copy-start.15
  19.2 7.3 copy-start.16
  19.2 7.3 copy-start.17
  19.2 7.3 copy-start.1
  19.2 7.3 copy-start.2
  26.8 11.9 copy-start
  40.4 467.7 %all-gather.19.cloned.1.call-start = ((), (), s32[]{:S(2)}) async-start(), calls=%async_computation.4 | async-start | bytes 32849920 | tf_op jit(solution)/shard_map/all_gather | solution.py:767
  40.5 234.1 %copy-start.9 = (s32[32,128]{1,0:T(8,128)S(1)}, s32[32,128]{1,0:T(8,128)}, u32[]{:S(2)}) copy-start(s32[32,128]{1,0:T(8,128)} %param.19) | copy-start | bytes 49156
  40.5 234.6 %copy-start.11 = (bf16[4096]{0:T(1024)(128)(2,1)S(1)}, bf16[4096]{0:T(1024)(128)(2,1)}, u32[]{:S(2)}) copy-start(bf16[4096]{0:T(1024)(128)(2,1)} %param.20) | copy-start | bytes 24580
  41.2 700.0 %all-gather.17.cloned.1.call-start = ((), (), s32[]{:S(2)}) async-start(), calls=%async_computation.3 | async-start | bytes 32849920 | tf_op jit(solution)/shard_map/all_gather | solution.py:767
  41.9 934.2 %all-gather.15.cloned.1.call-start = ((), (), s32[]{:S(2)}) async-start(), calls=%async_computation.2 | async-start | bytes 32849920 | tf_op jit(solution)/shard_map/all_gather | solution.py:767
  42.5 2241.7 %all-gather.13.cloned.1.call-start = ((), (), s32[]{:S(2)}) async-start(), calls=%async_computation.1 | async-start | bytes 31457280 | tf_op jit(solution)/shard_map/all_gather | solution.py:807
  274.6 707.9 %collective-permute-start.4 = (f32[4,6416,256]{2,1,0:T(8,128)}, f32[4,6416,256]{2,1,0:T(8,128)}, u32[]{:S(2)}, u32[]{:S(2)}) collective-permute-start(f32[4,6416,256]{2,1,0:T(8,128)} %bitcast.132), channel_id=1, source_target_pairs={{0,1},{1,0},{2,3},{3,2},{4,5},{5,4},{6,7},{7,6}} | collective-permute-start | bytes 78839816 | tf_op jit(solution)/shard_map/ppermute | solution.py:770
  274.6 66.5 %collective-permute-start.1 = (s32[32,8]{1,0:T(8,128)S(1)}, s32[32,8]{1,0:T(8,128)S(1)}, u32[]{:S(2)}, u32[]{:S(2)}) collective-permute-start(s32[32,8]{1,0:T(8,128)S(1)} %bitcast.118), channel_id=1, source_target_pairs={{0,1},{1,0},{2,3},{3,2},{4,5},{5,4},{6,7},{7,6}} | collective-permute-start | bytes 3080 | tf_op jit(solution)/shard_map/ppermute | solution.py:770
  508.1 640.1 %collective-permute-start.3 = (f32[4,6416,256]{2,1,0:T(8,128)}, f32[4,6416,256]{2,1,0:T(8,128)}, u32[]{:S(2)}, u32[]{:S(2)}) collective-permute-start(f32[4,6416,256]{2,1,0:T(8,128)} %bitcast.129), channel_id=1, source_target_pairs={{0,1},{1,0},{2,3},{3,2},{4,5},{5,4},{6,7},{7,6}} | collective-permute-start | bytes 78839816 | tf_op jit(solution)/shard_map/ppermute | solution.py:770
  741.2 570.3 %collective-permute-start.2 = (f32[4,6416,256]{2,1,0:T(8,128)}, f32[4,6416,256]{2,1,0:T(8,128)}, u32[]{:S(2)}, u32[]{:S(2)}) collective-permute-start(f32[4,6416,256]{2,1,0:T(8,128)} %bitcast.126), channel_id=1, source_target_pairs={{0,1},{1,0},{2,3},{3,2},{4,5},{5,4},{6,7},{7,6}} | collective-permute-start | bytes 78839816 | tf_op jit(solution)/shard_map/ppermute | solution.py:770
  976.1 498.4 %collective-permute-start = (f32[4,6416,256]{2,1,0:T(8,128)}, f32[4,6416,256]{2,1,0:T(8,128)}, u32[]{:S(2)}, u32[]{:S(2)}) collective-permute-start(f32[4,6416,256]{2,1,0:T(8,128)} %bitcast.123), channel_id=1, source_target_pairs={{0,1},{1,0},{2,3},{3,2},{4,5},{5,4},{6,7},{7,6}} | collective-permute-start | bytes 78839816 | tf_op jit(solution)/shard_map/ppermute | solution.py:770
  1675.7 640.9 %all-gather.11.cloned.1.call-start = ((), (), s32[]{:S(2)}) async-start(), calls=%async_computation | async-start | bytes 20971520 | tf_op jit(solution)/shard_map/all_gather | solution.py:807
  1675.8 91.4 %slice-start = ((s8[8388608]{0:T(1024)(128)(4,1)}), s8[4194304]{0:T(1024)(128)(4,1)S(1)}, s32[]{:S(2)}) async-start(s8[8388608]{0:T(1024)(128)(4,1)} %bitcast.135), calls=%async_computation.6 | async-start | bytes 8388608
  1721.7 120.6 %collective-permute-start.6 = (f32[4096,1024]{1,0:T(8,128)}, f32[4096,1024]{1,0:T(8,128)}, u32[]{:S(2)}, u32[]{:S(2)}) collective-permute-start(f32[4096,1024]{1,0:T(8,128)} %fusion.18), channel_id=1, source_target_pairs={{0,1},{1,0},{2,3},{3,2},{4,5},{5,4},{6,7},{7,6}} | collective-permute-start | bytes 50331656 | tf_op jit(solution)/shard_map/ppermute | solution.py:770
  1721.9 45.3 %slice-start.1 = ((s8[8388608]{0:T(1024)(128)(4,1)}), s8[4194304]{0:T(1024)(128)(4,1)S(1)}, s32[]{:S(2)}) async-start(s8[8388608]{0:T(1024)(128)(4,1)} %bitcast.135), calls=%async_computation.7 | async-start | bytes 8388608
  1766.8 92.8 %collective-permute-start.7 = (f32[4096,1024]{1,0:T(8,128)}, f32[4096,1024]{1,0:T(8,128)}, u32[]{:S(2)}, u32[]{:S(2)}) collective-permute-start(f32[4096,1024]{1,0:T(8,128)} %fusion.19), channel_id=1, source_target_pairs={{0,1},{1,0},{2,3},{3,2},{4,5},{5,4},{6,7},{7,6}} | collective-permute-start | bytes 50331656 | tf_op jit(solution)/shard_map/ppermute | solution.py:770
  1810.2 66.5 %collective-permute-start.9 = (f32[1024,4096]{1,0:T(8,128)}, f32[1024,4096]{1,0:T(8,128)}, u32[]{:S(2)}, u32[]{:S(2)}) collective-permute-start(f32[1024,4096]{1,0:T(8,128)} %fusion.20), channel_id=1, source_target_pairs={{0,1},{1,0},{2,3},{3,2},{4,5},{5,4},{6,7},{7,6}} | collective-permute-start | bytes 50331656 | tf_op jit(solution)/shard_map/ppermute | solution.py:770
  1810.5 12.0 copy-start.7
  1810.5 12.6 copy-start.12
  1810.5 13.2 copy-start.4
  1822.2 16.5 collective-permute-start.8
  2284.2 30.9 %copy-start.3 = (f32[10,2,4,128]{3,1,2,0:T(2,128)S(1)}, f32[10,2,4,128]{3,1,2,0:T(2,128)}, u32[]{:S(2)}) copy-start(f32[10,2,4,128]{3,1,2,0:T(2,128)} %copy.105) | copy-start | bytes 122884
  2316.4 15.0 collective-permute-start.5
  (4 other events, 17.2 us)
Sparse Core Ops, SparseCore 0:
  40.5 233.9 all-gather.20
  276.9 231.1 all-gather.18
  509.9 231.1 all-gather.16
  742.8 231.1 all-gather.14
  1675.8 222.1 all-gather.12
  1912.3 151.8 all-gather.10

commit v4 on v3

--- a/solution.py
+++ b/solution.py
@@ -49,7 +49,7 @@
 
 
 NTOK, WIDE = TOK // TILE, 512
-FULL_DN, FULL_Z = 20 * SUB * TILE, 24 * SUB * TILE
+FULL_DN, FULL_Z = 18 * SUB * TILE, 24 * SUB * TILE
 NBLK = GRP * NTOK
 ONE_ROW = pl.BlockSpec((1, DM), lambda i: (0, 0))
 SUM_BLOCK = pl.BlockSpec((SUB, DM), lambda i: (0, 0))
@@ -149,13 +149,11 @@
 
 
 def proj_call(rows, acts, weight, x, b_out):
-    tok = WIDE // SUB
-    per = TOK // tok
-    seq = pl.BlockSpec((SUB, tok, WIDE), lambda n, m: (m // per, m % per, n))
+    seq = pl.BlockSpec((SUB, TOK, WIDE), lambda n, m: (m, 0, n))
     return pl.pallas_call(
-        proj_kernel, grid=(DM // WIDE, rows // WIDE),
-        in_specs=[pl.BlockSpec((WIDE, DM), lambda n, m: (m, 0)), pl.BlockSpec((WIDE, DM), lambda n, m: (n, 0)), seq, pl.BlockSpec((1, WIDE), lambda n, m: (0, n))],
-        out_specs=seq, out_shape=sds((GRP * SUB, TOK, DM), BF), scratch_shapes=[pltpu.VMEM((WIDE // LANES, WIDE, LANES), F32)],
+        proj_kernel, grid=(DM // WIDE, rows // GROWS),
+        in_specs=[pl.BlockSpec((GROWS, DM), lambda n, m: (m, 0)), pl.BlockSpec((WIDE, DM), lambda n, m: (n, 0)), seq, pl.BlockSpec((1, WIDE), lambda n, m: (0, n))],
+        out_specs=seq, out_shape=sds((GRP * SUB, TOK, DM), BF), scratch_shapes=[pltpu.VMEM((WIDE // LANES, GROWS, LANES), F32)],
         compiler_params=params(), cost_estimate=cost(130), name="proj_z")(acts, weight, x, b_out)
 
 

time: 2350 us -> 2320 us (0.987)
  transfers between devices with their start and end apart: 16 -> 16, of which waited for: 4 -> 4; matrix products, arithmetic and copies ran while one was open for 18% -> 17% of each run, Pallas kernels for 44% -> 44%
where the time goes in v4:
time: 2320 us; the launch traced here: 2310 us
  Pallas kernels  1170 us (50%)
  waiting for transfers between devices  647 us (28%)
  matrix products  370 us (16%)
  other arithmetic  78.8 us (3%)
  local copies, waits for them, and re-layouts  27.3 us (1%)
    pallas_call x5, Pallas kernels, rnn_call(): pl.pallas_call(functools.partial(rnn_kernel, own, groups, units, chip_of,...  888 us
    all_gather x4, waiting for transfers between devices, layer(): got.append(lax.all_gather(mine, 'tp'))  631 us
    dot_general x6, matrix products, dot(): return lax.dot_general(lhs, rhs, dims, preferred_element_type=F32)  358 us
    pallas_call x4, Pallas kernels, row_call(): pl.pallas_call(kernel, grid=(last - first,), in_specs=in_specs, out_specs...  157 us
    pallas_call x1, Pallas kernels, proj_call(): pl.pallas_call(proj_kernel, grid=(DM // WIDE, rows // GROWS), in_specs=[p...  126 us
    add x5, other arithmetic, merged(): return val + theirs  55.3 us
  transfers between devices with their start and end apart: 16, of which 4 were waited for; matrix products, arithmetic and copies ran while one was open for 17% of the time, Pallas kernels for 44%

profile of v4, /device:TPU:0, one launch (start us, length us, event | category | flops | bytes accessed | tf_op | source)
XLA Modules:
  0.0 2311.5 jit_solution(4884268885427699351)
XLA Ops:
  7.2 11.9 copy.96
  19.2 5.8 convert_dynamic-update-slice_fusion.1
  26.8 6.5 convert_dynamic-update-slice_fusion
  33.3 5.4 bitcast_dynamic-update-slice_fusion.1
  43.1 231.5 %all-gather.21.cloned.1.call-done = f32[25664,256]{1,0:T(8,128)} async-done(((f32[6416,256]{1,0:T(8,128)}), f32[25664,256]{1,0:T(8,128)}) %all-gather.21.cloned.1.call-update) | async-done | bytes 26279952 | tf_op jit(solution)/shard_map/all_gather | solution.py:765
  275.7 65.4 %shard_map.288 = (bf16[4096,4096]{1,0:T(8,128)(2,1)}, bf16[4096,4096]{1,0:T(8,128)(2,1)}, f32[8,4096]{1,0:T(8,128)}) custom-call(bf16[32,128,4096]{2,1,0:T(8,128)(2,1)} %x_ref.9, bf16[32,128,4096]{2,1,0:T(8,128)(2,1)} %gz_ref.5, f32[1,4096]{1,0:T(1,128)} %bitcast.113), custom_call_target="tpu_custom_call" | custom-call | flops 60000002048 | bytes 60000000 | tf_op jit(solution)/shard_map/pallas_call | solution.py:70
  341.4 166.7 %all-gather.19.cloned.1.call-done = f32[25664,256]{1,0:T(8,128)} async-done(((f32[6416,256]{1,0:T(8,128)}), f32[25664,256]{1,0:T(8,128)}) %all-gather.19.cloned.1.call-update) | async-done | bytes 26279952 | tf_op jit(solution)/shard_map/all_gather | solution.py:765
  508.1 233.0 %all-gather.17.cloned.1.call-done = f32[25664,256]{1,0:T(8,128)} async-done(((f32[6416,256]{1,0:T(8,128)}), f32[25664,256]{1,0:T(8,128)}) %all-gather.17.cloned.1.call-update) | async-done | bytes 26279952 | tf_op jit(solution)/shard_map/all_gather | solution.py:765
  741.2 2.0 broadcast_in_dim.41.refs_7_.refs_5_
  743.2 232.9 %shard_map.289 = (bf16[4096,4096]{1,0:T(8,128)(2,1)}, bf16[4096,8192]{1,0:T(8,128)(2,1)}, bf16[4096,8192]{1,0:T(8,128)(2,1)}, bf16[4096,4096]{1,0:T(8,128)(2,1)}...) custom-call(bf16[4096,4096]{1,0:T(8,128)(2,1)} %get-tuple-element.49, ...), custom_call_target="tpu_custom_call" | custom-call | flops 160000000000 | bytes 160000000 | tf_op jit(solution)/shard_map/pallas_call | solution.py:737
  976.5 1.5 slice_bitcast_fusion.refs_4_
  982.4 165.9 %shard_map.290 = (bf16[4096,4096]{1,0:T(8,128)(2,1)}, bf16[4096,8192]{1,0:T(8,128)(2,1)}, bf16[4096,8192]{1,0:T(8,128)(2,1)}, bf16[4096,4096]{1,0:T(8,128)(2,1)}) custom-call(bf16[4096,4096]{1,0:T(8,128)(2,1)} %get-tuple-element.49.refs_0_, ...), custom_call_target="tpu_custom_call", output_to_operand_aliasing={{0}: (6, {}), {1}: (7, {}), {2}: (8, {}), {3}: (9, {})} | custom-call | flops 120000004096 | bytes 120000000 | tf_op jit(solution)/shard_map/pallas_call | solution.py:737
  1148.3 163.1 %shard_map.291 = (bf16[4096,4096]{1,0:T(8,128)(2,1)}, bf16[4096,8192]{1,0:T(8,128)(2,1)}, bf16[4096,8192]{1,0:T(8,128)(2,1)}, bf16[4096,4096]{1,0:T(8,128)(2,1)}) custom-call(bf16[4096,4096]{1,0:T(8,128)(2,1)} %get-tuple-element.49.refs_0_, ...), custom_call_target="tpu_custom_call", output_to_operand_aliasing={{0}: (6, {}), {1}: (7, {}), {2}: (8, {}), {3}: (9, {})} | custom-call | flops 120000004096 | bytes 120000000 | tf_op jit(solution)/shard_map/pallas_call | solution.py:737
  1311.4 163.1 %shard_map.292 = (bf16[4096,4096]{1,0:T(8,128)(2,1)}, bf16[4096,8192]{1,0:T(8,128)(2,1)}, bf16[4096,8192]{1,0:T(8,128)(2,1)}, bf16[4096,4096]{1,0:T(8,128)(2,1)}) custom-call(bf16[4096,4096]{1,0:T(8,128)(2,1)} %get-tuple-element.49.refs_0_, ...), custom_call_target="tpu_custom_call", output_to_operand_aliasing={{0}: (6, {}), {1}: (7, {}), {2}: (8, {}), {3}: (9, {})} | custom-call | flops 120000004096 | bytes 120000000 | tf_op jit(solution)/shard_map/pallas_call | solution.py:737
  1474.6 163.3 %shard_map.293 = (bf16[4096,4096]{1,0:T(8,128)(2,1)}, bf16[4096,8192]{1,0:T(8,128)(2,1)}, bf16[4096,8192]{1,0:T(8,128)(2,1)}, bf16[4096,4096]{1,0:T(8,128)(2,1)}) custom-call(bf16[4096,4096]{1,0:T(8,128)(2,1)} %get-tuple-element.49.refs_0_, ...), custom_call_target="tpu_custom_call", output_to_operand_aliasing={{0}: (6, {}), {1}: (7, {}), {2}: (8, {}), {3}: (9, {})} | custom-call | flops 120000004096 | bytes 120000000 | tf_op jit(solution)/shard_map/pallas_call | solution.py:737
  1637.9 38.5 %fusion.2 = f32[448,4096]{1,0:T(8,128)} fusion(bf16[4096,8192]{1,0:T(8,128)(2,1)} %get-tuple-element.70, bf16[4096,8192]{1,0:T(8,128)(2,1)} %get-tuple-element.69, s32[]{:T(128)S(6)} %select_n.42), kind=kOutput, calls=%fused_computation.2 | convolution fusion | flops 30064771072 | bytes 81788928 | tf_op jit(solution)/shard_map/dot_general | solution.py:782
  1676.6 46.4 %fusion.18 = f32[4096,1024]{1,0:T(8,128)} fusion(bf16[4096,4096]{1,0:T(8,128)(2,1)} %get-tuple-element.49.refs_0_, bf16[4096,1024]{1,0:T(8,128)(2,1)} %get-tuple-element.77), kind=kOutput, calls=%fused_computation.61 | convolution fusion | flops 34359738368 | bytes 58720256 | tf_op jit(solution)/shard_map/dot_general | solution.py:782
  1723.1 44.2 %fusion.19 = f32[4096,1024]{1,0:T(8,128)} fusion(bf16[4096,4096]{1,0:T(8,128)(2,1)} %get-tuple-element.49.refs_0_, bf16[4096,1024]{1,0:T(8,128)(2,1)} %get-tuple-element.78), kind=kOutput, calls=%fused_computation.62 | convolution fusion | flops 34359738368 | bytes 58720256 | tf_op jit(solution)/shard_map/dot_general | solution.py:782
  1767.7 42.5 %fusion.20 = f32[1024,4096]{1,0:T(8,128)} fusion(bf16[4096,1024]{1,0:T(8,128)(2,1)S(1)} %bitcast.136, bf16[4096,4096]{1,0:T(8,128)(2,1)} %get-tuple-element.50.refs_1_), kind=kOutput, calls=%fused_computation.63 | convolution fusion | flops 34359738368 | bytes 58720256 | tf_op jit(solution)/shard_map/dot_general | solution.py:782
  1810.3 11.7 convolution_multiply_fusion
  1824.5 14.2 collective-permute-done.8
  1838.7 2.1 add.62
  1840.8 1.5 fusion.15
  1842.3 17.3 add.60
  1859.6 17.1 add.61
  1876.7 17.9 add.64
  1894.6 17.5 fusion.4
  1912.1 168.8 %fusion.dn_ref = f32[2304,4096]{1,0:T(8,128)} fusion(bf16[4096,8192]{1,0:T(8,128)(2,1)} %get-tuple-element.70, bf16[4096,8192]{1,0:T(8,128)(2,1)} %get-tuple-element.69), kind=kOutput, calls=%fused_computation | convolution fusion | flops 154618822656 | bytes 142606336 | tf_op jit(solution)/shard_map/dot_general | solution.py:782
  2080.9 42.8 %shard_map.295 = (bf16[32,128,4096]{2,1,0:T(8,128)(2,1)}, f32[8,4096]{1,0:T(8,128)}) custom-call(f32[2304,4096]{1,0:T(8,128)} %fusion.dn_ref, bf16[32,128,4096]{2,1,0:T(8,128)(2,1)} %x_ref.9, bf16[32,128,4096]{2,1,0:T(8,128)(2,1)} %gz_ref.5, f32[1,4096]{1,0:T(1,128)} %bitcast.114), custom_call_target="tpu_custom_call" | custom-call | flops 49999998976 | bytes 50000000 | tf_op jit(solution)/shard_map/pallas_call | solution.py:70
  2123.7 125.6 %proj_z.1.refs_0_ = bf16[32,128,4096]{2,1,0:T(8,128)(2,1)} custom-call(bf16[4096,4096]{1,0:T(8,128)(2,1)} %get-tuple-element.67.act_ref, bf16[4096,4096]{1,0:T(8,128)(2,1)} %get-tuple-element.68.w_ref, bf16[32,128,4096]{2,1,0:T(8,128)(2,1)} %x_ref.9, f32[1,4096]{1,0:T(1,128)} %bitcast.116), custom_call_target="tpu_custom_call" | custom-call | flops 130000003072 | bytes 130000000 | tf_op jit(solution)/shard_map/proj_z/pallas_call | solution.py:153
  2249.3 33.7 %shard_map.296 = (bf16[32,128,4096]{2,1,0:T(8,128)(2,1)}, f32[8,4096]{1,0:T(8,128)}) custom-call(f32[1792,4096]{1,0:T(8,128)} %all-gather.13.cloned.1.call-done.dn_ref, bf16[32,128,4096]{2,1,0:T(8,128)(2,1)} %x_ref.9, bf16[32,128,4096]{2,1,0:T(8,128)(2,1)} %gz_ref.5, f32[1,4096]{1,0:T(1,128)} %bitcast.115, ...), custom_call_target="tpu_custom_call", output_to_operand_aliasing={{0}: (4, {})} | custom-call | flops 49999998976 | bytes 50000000 | tf_op jit(solution)/shard_map/pallas_call | solution.py:70
  2286.2 14.8 shard_map.294
  (108 shorter events, 21.9 us)
Async XLA Ops:
  7.2 267.4 %all-gather.21.cloned.1.call-start = ((), (), s32[]{:S(2)}) async-start(), calls=%async_computation.5 | async-start | bytes 32849920 | tf_op jit(solution)/shard_map/all_gather | solution.py:765
  19.2 7.2 copy-start.14
  19.2 7.3 copy-start.10
  19.2 7.3 copy-start.15
  19.2 7.3 copy-start.16
  19.2 7.3 copy-start.17
  19.2 7.3 copy-start.1
  19.2 7.3 copy-start.2
  26.8 11.9 copy-start
  40.4 467.7 %all-gather.19.cloned.1.call-start = ((), (), s32[]{:S(2)}) async-start(), calls=%async_computation.4 | async-start | bytes 32849920 | tf_op jit(solution)/shard_map/all_gather | solution.py:765
  40.5 234.1 %copy-start.9 = (s32[32,128]{1,0:T(8,128)S(1)}, s32[32,128]{1,0:T(8,128)}, u32[]{:S(2)}) copy-start(s32[32,128]{1,0:T(8,128)} %param.19) | copy-start | bytes 49156
  40.5 234.6 %copy-start.11 = (bf16[4096]{0:T(1024)(128)(2,1)S(1)}, bf16[4096]{0:T(1024)(128)(2,1)}, u32[]{:S(2)}) copy-start(bf16[4096]{0:T(1024)(128)(2,1)} %param.20) | copy-start | bytes 24580
  41.2 700.0 %all-gather.17.cloned.1.call-start = ((), (), s32[]{:S(2)}) async-start(), calls=%async_computation.3 | async-start | bytes 32849920 | tf_op jit(solution)/shard_map/all_gather | solution.py:765
  41.9 934.2 %all-gather.15.cloned.1.call-start = ((), (), s32[]{:S(2)}) async-start(), calls=%async_computation.2 | async-start | bytes 32849920 | tf_op jit(solution)/shard_map/all_gather | solution.py:765
  42.5 2206.8 %all-gather.13.cloned.1.call-start = ((), (), s32[]{:S(2)}) async-start(), calls=%async_computation.1 | async-start | bytes 36700160 | tf_op jit(solution)/shard_map/all_gather | solution.py:805
  274.6 707.9 %collective-permute-start.4 = (f32[4,6416,256]{2,1,0:T(8,128)}, f32[4,6416,256]{2,1,0:T(8,128)}, u32[]{:S(2)}, u32[]{:S(2)}) collective-permute-start(f32[4,6416,256]{2,1,0:T(8,128)} %bitcast.132), channel_id=1, source_target_pairs={{0,1},{1,0},{2,3},{3,2},{4,5},{5,4},{6,7},{7,6}} | collective-permute-start | bytes 78839816 | tf_op jit(solution)/shard_map/ppermute | solution.py:768
  274.6 66.5 %collective-permute-start.1 = (s32[32,8]{1,0:T(8,128)S(1)}, s32[32,8]{1,0:T(8,128)S(1)}, u32[]{:S(2)}, u32[]{:S(2)}) collective-permute-start(s32[32,8]{1,0:T(8,128)S(1)} %bitcast.118), channel_id=1, source_target_pairs={{0,1},{1,0},{2,3},{3,2},{4,5},{5,4},{6,7},{7,6}} | collective-permute-start | bytes 3080 | tf_op jit(solution)/shard_map/ppermute | solution.py:768
  508.1 640.1 %collective-permute-start.3 = (f32[4,6416,256]{2,1,0:T(8,128)}, f32[4,6416,256]{2,1,0:T(8,128)}, u32[]{:S(2)}, u32[]{:S(2)}) collective-permute-start(f32[4,6416,256]{2,1,0:T(8,128)} %bitcast.129), channel_id=1, source_target_pairs={{0,1},{1,0},{2,3},{3,2},{4,5},{5,4},{6,7},{7,6}} | collective-permute-start | bytes 78839816 | tf_op jit(solution)/shard_map/ppermute | solution.py:768
  741.2 570.3 %collective-permute-start.2 = (f32[4,6416,256]{2,1,0:T(8,128)}, f32[4,6416,256]{2,1,0:T(8,128)}, u32[]{:S(2)}, u32[]{:S(2)}) collective-permute-start(f32[4,6416,256]{2,1,0:T(8,128)} %bitcast.126), channel_id=1, source_target_pairs={{0,1},{1,0},{2,3},{3,2},{4,5},{5,4},{6,7},{7,6}} | collective-permute-start | bytes 78839816 | tf_op jit(solution)/shard_map/ppermute | solution.py:768
  976.1 498.4 %collective-permute-start = (f32[4,6416,256]{2,1,0:T(8,128)}, f32[4,6416,256]{2,1,0:T(8,128)}, u32[]{:S(2)}, u32[]{:S(2)}) collective-permute-start(f32[4,6416,256]{2,1,0:T(8,128)} %bitcast.123), channel_id=1, source_target_pairs={{0,1},{1,0},{2,3},{3,2},{4,5},{5,4},{6,7},{7,6}} | collective-permute-start | bytes 78839816 | tf_op jit(solution)/shard_map/ppermute | solution.py:768
  1676.5 609.7 %all-gather.11.cloned.1.call-start = ((), (), s32[]{:S(2)}) async-start(), calls=%async_computation | async-start | bytes 20971520 | tf_op jit(solution)/shard_map/all_gather | solution.py:805
  1676.6 91.1 %slice-start = ((s8[8388608]{0:T(1024)(128)(4,1)}), s8[4194304]{0:T(1024)(128)(4,1)S(1)}, s32[]{:S(2)}) async-start(s8[8388608]{0:T(1024)(128)(4,1)} %bitcast.135), calls=%async_computation.6 | async-start | bytes 8388608
  1723.0 119.3 %collective-permute-start.6 = (f32[4096,1024]{1,0:T(8,128)}, f32[4096,1024]{1,0:T(8,128)}, u32[]{:S(2)}, u32[]{:S(2)}) collective-permute-start(f32[4096,1024]{1,0:T(8,128)} %fusion.18), channel_id=1, source_target_pairs={{0,1},{1,0},{2,3},{3,2},{4,5},{5,4},{6,7},{7,6}} | collective-permute-start | bytes 50331656 | tf_op jit(solution)/shard_map/ppermute | solution.py:768
  1723.1 44.6 %slice-start.1 = ((s8[8388608]{0:T(1024)(128)(4,1)}), s8[4194304]{0:T(1024)(128)(4,1)S(1)}, s32[]{:S(2)}) async-start(s8[8388608]{0:T(1024)(128)(4,1)} %bitcast.135), calls=%async_computation.7 | async-start | bytes 8388608
  1767.2 92.3 %collective-permute-start.7 = (f32[4096,1024]{1,0:T(8,128)}, f32[4096,1024]{1,0:T(8,128)}, u32[]{:S(2)}, u32[]{:S(2)}) collective-permute-start(f32[4096,1024]{1,0:T(8,128)} %fusion.19), channel_id=1, source_target_pairs={{0,1},{1,0},{2,3},{3,2},{4,5},{5,4},{6,7},{7,6}} | collective-permute-start | bytes 50331656 | tf_op jit(solution)/shard_map/ppermute | solution.py:768
  1810.2 66.5 %collective-permute-start.9 = (f32[1024,4096]{1,0:T(8,128)}, f32[1024,4096]{1,0:T(8,128)}, u32[]{:S(2)}, u32[]{:S(2)}) collective-permute-start(f32[1024,4096]{1,0:T(8,128)} %fusion.20), channel_id=1, source_target_pairs={{0,1},{1,0},{2,3},{3,2},{4,5},{5,4},{6,7},{7,6}} | collective-permute-start | bytes 50331656 | tf_op jit(solution)/shard_map/ppermute | solution.py:768
  1810.3 12.2 copy-start.7
  1810.3 12.8 copy-start.12
  1810.3 13.4 copy-start.4
  1822.0 16.7 collective-permute-start.8
  2249.3 35.3 %copy-start.3 = (f32[10,2,4,128]{3,1,2,0:T(2,128)S(1)}, f32[10,2,4,128]{3,1,2,0:T(2,128)}, u32[]{:S(2)}) copy-start(f32[10,2,4,128]{3,1,2,0:T(2,128)} %copy.105) | copy-start | bytes 122884
  2286.0 15.0 collective-permute-start.5
  (4 other events, 17.2 us)
Sparse Core Ops, SparseCore 0:
  40.5 233.9 all-gather.20
  276.9 231.1 all-gather.18
  509.9 231.1 all-gather.16
  742.8 231.1 all-gather.14
  1676.6 256.5 all-gather.12
  1934.9 151.7 all-gather.10
